TPU v7x, 32 devices: a whole 2x2x4 slice. The times are simulated.
32 devices in a mesh: blk: 16 (over z, y, x), phe: 2 (over core).
Axes of the slice: x: 2, y: 2, z: 4, core: 2. Of those that a mesh axis runs over, the one named last changes fastest.
Arguments:
- ld_rows: bfloat16 [16384, 1024], P('blk'), may hold values from -1.5 to 1.5, as said below
- block_first: int32 [16384], P('blk'), may hold values from 0 to 16383, as said below
- beta_hat: float32 [128, 16384], P('phe', 'blk'), may hold values from -6 to 6
- psi: float32 [128, 16384], P('phe', 'blk'), may hold values from 0.05 to 5
- noise: bfloat16 [3, 128, 16384], P(None, 'phe', 'blk'), may hold values from -5 to 5
- sample_size: int32 [128], P('phe'), may hold values from 2000 to 199999
Outputs:
- effects: float32 [128, 16384], P('phe', 'blk')
Inputs may be any that keep to these rules, and one draw needn't show every extreme that they name: block_first[j] is the first SNP of the run of consecutive SNPs that forms j's LD block; every block holds 128 to 1024 SNPs, except the last block, which ends at SNP 16384 - 1 and may hold fewer. ld_rows[j, c] is the LD between SNP j and SNP block_first[j] + c for c below the length of j's block, and zero for larger c; every block's matrix is symmetric with unit diagonal.
All inputs are finite; a program needn't handle non-finite values.
Results may differ from a plain program's by a relative error of at most 0.00055.
The roundings to bfloat16 on the way count: a program that leaves them out, or rounds other values in their place, can miss the bound.
Values may be sent and summed in bfloat16 or wider, within the bound.
No kernel may reach another device: no remote copies, remote signals or barrier semaphores. Data moves between devices by JAX's collectives and lax.ppermute only.
A program may use at most 64 MiB of HBM per device.

v0:
```python
import functools

import jax
import jax.numpy as jnp
from jax import lax
from jax.experimental import pallas as pl
from jax.experimental.pallas import tpu as pltpu
from jax.sharding import PartitionSpec as P


ITERS = 3
LANES = 128
TILE = 256
WINDOWS = 3

tiny_term = 1e-06
sample_ref = 20000.0


def chunk_sums(values):
    total = values[:, :LANES]
    for at in range(LANES, values.shape[1], LANES):
        total = total + values[:, at : at + LANES]
    return total


def spread(resid, scale, out_ref):
    both = jnp.concatenate([chunk_sums(resid), chunk_sums(scale)], axis=0)
    row = jnp.sum(both.T, axis=0, keepdims=True)
    out_ref[...] = jnp.broadcast_to(row, out_ref.shape)


def first_sums(beta_hat_ref, kept_ref, out_ref, sem):
    copy = pltpu.make_async_copy(beta_hat_ref, kept_ref, sem)
    copy.start()
    copy.wait()
    grad = kept_ref[...]
    spread(grad * grad, jnp.zeros_like(grad), out_ref)


def load(block_first_ref, psi_ref, noise_ref, ld_ref, psi_out, noise_out, ld_out, table_ref, starts, sems):
    pairs = (block_first_ref, starts), (psi_ref, psi_out), (noise_ref, noise_out), (ld_ref, ld_out)
    copies = [pltpu.make_async_copy(a, b, sems.at[n]) for n, (a, b) in enumerate(pairs)]
    for copy in copies:
        copy.start()
    copies[0].wait()
    first = starts[...]
    row = lax.broadcasted_iota(jnp.int32, first.shape, 0) * 2
    lane = lax.broadcasted_iota(jnp.int32, first.shape, 1)
    start = jnp.where(lane == row, jnp.broadcast_to(first[:, :1], first.shape), 0)
    end = jnp.where(lane == row + 1, jnp.broadcast_to(first[:, LANES - 1 :], first.shape), 0)
    table_ref[...] = jnp.sum(start + end, axis=0, keepdims=True)
    for copy in copies[1:]:
        copy.wait()


def update(own, groups, snps, sums_ref, sample_size_ref, value_ref, psi_ref, noise_ref, beta_ref, low_ref=None):
    sums = sums_ref[...]
    half = sums.shape[1] // 2
    member = lax.rem(lax.broadcasted_iota(jnp.int32, sums.shape, 0), groups) == lax.axis_index(own)
    mine = jnp.sum(jnp.where(member, sums, 0.0), axis=0, keepdims=True)
    every = jnp.sum(sums, axis=0, keepdims=True)
    lane = lax.broadcasted_iota(jnp.int32, every.shape, 1)
    pooled = jnp.sum(jnp.where(lane >= half, every, 0.0), axis=1, keepdims=True)
    pooled = pooled / (snps * groups * half) + tiny_term
    mean = mine / snps + tiny_term
    samples = sample_size_ref[...].astype(jnp.float32)
    amp = jnp.sqrt(mean * sample_ref / jnp.concatenate([samples, samples], axis=1))
    phi = (mean + pooled) / 2.0
    table = jnp.broadcast_to(jnp.where(lane >= half, phi, amp), (2 * half, 2 * half)).T
    amp, phi = table[:half, :LANES], table[half:, :LANES]
    for at in range(0, psi_ref.shape[1], LANES):
        cut = slice(at, at + LANES)
        psi = psi_ref[:, cut]
        beta = psi / (psi + phi) * (value_ref[:, cut] + amp * noise_ref[0, :, cut].astype(jnp.float32))
        beta_ref[:, cut] = beta
        if low_ref is not None:
            low_ref[:, cut] = beta.astype(jnp.bfloat16)


def gradient(along, firsts_ref, far_ref, low_ref, near_ref, ld_ref, beta_hat_ref, psi_ref, beta_ref, value_ref, out_ref, wide, windows):
    rows, span = ld_ref.shape
    phenos = low_ref.shape[0]
    place = lax.axis_index(along)
    base = place * rows
    odd = lax.rem(place, 2)
    tiles = rows // TILE
    steps = 2 * TILE // LANES
    for third, part in ((0, far_ref), (1, low_ref), (2, near_ref)):
        at = pl.multiple_of(jnp.where(odd == 1, 2 - third, third) * span, LANES)
        wide[:, pl.ds(at, span)] = part[...]
    lane = lax.broadcasted_iota(jnp.int32, (phenos, LANES), 1)

    def fill(slot, first):
        start = first - base + span
        whole = pl.multiple_of(lax.div(start, LANES) * LANES, LANES)
        rest = start - whole
        turn = lax.rem(LANES - rest, LANES)
        keep = lane < LANES - rest
        now = pltpu.roll(wide[:, pl.ds(whole, LANES)].astype(jnp.float32), turn, 1)
        for at in range(0, span, LANES):
            after = pltpu.roll(wide[:, pl.ds(pl.multiple_of(whole + at + LANES, LANES), LANES)].astype(jnp.float32), turn, 1)
            windows[slot, :, at : at + LANES] = jnp.where(keep, now, after).astype(jnp.bfloat16)
            now = after

    slot = 0
    before = firsts_ref[0, 0]
    fill(0, before)
    slots = []
    for number in range(tiles * steps):
        if number:
            first = firsts_ref[0, number]
            fresh = first != before
            slot = slot + fresh.astype(jnp.int32)

            @pl.when(fresh)
            def _(slot=slot, first=first):
                fill(slot, first)

            before = first
        slots.append((slot, before - base))

    resid = jnp.zeros((phenos, LANES), jnp.float32)
    scale = jnp.zeros((phenos, LANES), jnp.float32)
    for tile in range(tiles):
        cut = slice(tile * TILE, (tile + 1) * TILE)
        known = slots[tile * steps : (tile + 1) * steps]
        low = windows[pl.ds(known[0][0], WINDOWS)].reshape(WINDOWS * phenos, span)
        product = lax.dot_general(low, ld_ref[cut], (((1,), (1,)), ((), ())), preferred_element_type=jnp.float32)
        row = lax.broadcasted_iota(jnp.int32, (phenos, TILE), 1) + tile * TILE
        applied = product[:phenos]
        for turn in range(1, WINDOWS):
            begin = jnp.int32(rows)
            for other, where in reversed(known[1:]):
                begin = jnp.where(other == known[0][0] + turn, where, begin)
            applied = jnp.where(row >= begin, product[turn * phenos : (turn + 1) * phenos], applied)
        grad = beta_hat_ref[:, cut] - applied
        beta = beta_ref[:, cut]
        value_ref[:, cut] = beta + grad
        resid = resid + chunk_sums(grad * grad)
        scale = scale + chunk_sums(beta * beta / psi_ref[:, cut])
    spread(resid, scale, out_ref)


def shards(ld_rows, block_first, beta_hat, psi, noise, sample_size):
    rows, span = ld_rows.shape
    phenos = beta_hat.shape[0]
    blocks, groups = lax.axis_size("blk"), lax.axis_size("phe")
    snps = rows * blocks
    every = ("blk", "phe")
    vmem = pl.BlockSpec(memory_space=pltpu.VMEM)
    smem = pl.BlockSpec(memory_space=pltpu.SMEM)
    hbm = pl.BlockSpec(memory_space=pltpu.HBM)
    wide_shape = pltpu.VMEM(beta_hat.shape, jnp.float32)
    low_shape = pltpu.VMEM(beta_hat.shape, jnp.bfloat16)
    sums_shape = pltpu.VMEM((blocks * groups, 2 * phenos), jnp.float32)
    params = pltpu.CompilerParams(vmem_limit_bytes=16 << 20)

    def here(argument):
        return pltpu.with_memory_space_constraint(argument, pltpu.HBM)

    def total(sums):
        return lax.all_to_all(sums, every, 0, 0, tiled=True)

    beta_hat, sums = pl.pallas_call(
        first_sums,
        in_specs=[hbm],
        out_specs=[vmem] * 2,
        out_shape=[wide_shape, sums_shape],
        scratch_shapes=[pltpu.SemaphoreType.DMA],
        compiler_params=params,
    )(here(beta_hat))
    sums = total(sums)
    psi, noise, ld_rows, firsts = pl.pallas_call(
        load,
        in_specs=[hbm] * 4,
        out_specs=[vmem] * 4,
        out_shape=[wide_shape, pltpu.VMEM(noise.shape, noise.dtype), pltpu.VMEM(ld_rows.shape, ld_rows.dtype), pltpu.VMEM((1, LANES), jnp.int32)],
        scratch_shapes=[pltpu.VMEM((rows // LANES, LANES), jnp.int32), pltpu.SemaphoreType.DMA((4,))],
        compiler_params=params,
        cost_estimate=pl.CostEstimate(flops=1 << 24, bytes_accessed=3 << 20, transcendentals=0),
    )(*map(here, (block_first.reshape(-1, LANES), psi, noise, ld_rows)))

    def step(t, sums, value):
        last = t == ITERS - 1
        return pl.pallas_call(
            functools.partial(update, "phe", groups, snps),
            grid=(1,),
            in_specs=[vmem] * 4 + [pl.BlockSpec((1,) + beta_hat.shape, lambda i: (t, 0, 0))],
            out_specs=vmem if last else [vmem] * 2,
            out_shape=jax.ShapeDtypeStruct(beta_hat.shape, jnp.float32) if last else [wide_shape, low_shape],
            compiler_params=params,
        )(sums, sample_size[None], value, psi, noise)

    far = [(i, i + 1 if i % 2 else i - 1) for i in range(1, blocks - 1 + blocks % 2)]
    near = [(i, i ^ 1) for i in range(blocks - blocks % 2)]
    value = beta_hat
    for t in range(ITERS - 1):
        beta, low = step(t, sums, value)
        far_low = lax.ppermute(low, "blk", far)
        near_low = lax.ppermute(low, "blk", near)
        value, sums = pl.pallas_call(
            functools.partial(gradient, "blk"),
            in_specs=[smem] + [vmem] * 7,
            out_specs=[vmem] * 2,
            out_shape=[wide_shape, sums_shape],
            scratch_shapes=[
                pltpu.VMEM((phenos, 3 * span), jnp.bfloat16),
                pltpu.VMEM((2 * rows // LANES + WINDOWS, phenos, span), jnp.bfloat16),
            ],
            compiler_params=params,
        )(firsts, far_low, low, near_low, ld_rows, beta_hat, psi, beta)
        sums = total(sums)
    return step(ITERS - 1, sums, value)


def solution(mesh):
    in_specs = (
        P("blk", None),
        P("blk"),
        P("phe", "blk"),
        P("phe", "blk"),
        P(None, "phe", "blk"),
        P("phe"),
    )
    out_specs = P("phe", "blk")
    return jax.shard_map(shards, mesh=mesh, in_specs=in_specs, out_specs=out_specs, check_vma=False)
```

profile of v0, /device:TPU:0, one launch (start us, length us, event | category | flops | bytes accessed | tf_op | source)
XLA Modules:
  0.0 57.8 jit_solution(3636124035587307098)
XLA Ops:
  0.0 0.0 copy-start
  0.0 1.7 %shard_map.65 = (f32[64,1024]{1,0:T(8,128)S(1)}, f32[32,128]{1,0:T(8,128)}) custom-call(f32[64,1024]{1,0:T(8,128)} %beta_hat_ref.1), custom_call_target="tpu_custom_call" | custom-call | tf_op jit(solution)/shard_map/pallas_call | solution.py:165
  1.7 7.3 %all-to-all-start = ((f32[32,1,128]{2,1,0:T(1,128)}), f32[32,1,128]{2,1,0:T(1,128)S(1)}, u32[]{:S(2)}, u32[]{:S(2)}) async-start(f32[32,1,128]{2,1,0:T(1,128)} %bitcast.2), calls=%async_computation | async-start | bytes 32768 | tf_op jit(solution)/shard_map/all_to_all | solution.py:163
  9.0 1.9 %shard_map.64 = (f32[64,1024]{1,0:T(8,128)S(1)}, bf16[3,64,1024]{2,1,0:T(8,128)(2,1)S(1)}, bf16[1024,1024]{1,0:T(8,128)(2,1)S(1)}, s32[1,128]{1,0:T(1,128)S(1)}) custom-call(s32[8,128]{1,0:T(8,128)} %bitcast.22, f32[64,1024]{1,0:T(8,128)} %psi_ref.1, bf16[3,64,1024]{2,1,0:T(8,128)(2,1)} %noise_ref.1, bf16[1024,1024]{1,0:T(8,128)(2,1)} %ld_ref.1), custom_call_target="tpu_custom_call" | custom-call | flops 16777216 | bytes 3145728 | tf_op jit(solution)/shard_map/pallas_call | solution.py:174
  10.9 5.2 %all-to-all-done = f32[32,1,128]{2,1,0:T(1,128)S(1)} async-done(((f32[32,1,128]{2,1,0:T(1,128)}), f32[32,1,128]{2,1,0:T(1,128)S(1)}, u32[]{:S(2)}, u32[]{:S(2)}) %all-to-all-start) | async-done | bytes 16416 | tf_op jit(solution)/shard_map/all_to_all | solution.py:163
  16.1 0.0 copy-done
  16.1 0.2 shard_map.66
  16.4 0.6 %collective-permute-start.1 = (bf16[64,1024]{1,0:T(8,128)(2,1)S(1)}, bf16[64,1024]{1,0:T(8,128)(2,1)S(1)}, u32[]{:S(2)}, u32[]{:S(2)}) collective-permute-start(bf16[64,1024]{1,0:T(8,128)(2,1)S(1)} %get-tuple-element.24.low_ref), channel_id=1, source_target_pairs={{0,2},{2,0},{4,6},{6,4},{8,10},{10,8},{12,14},{14,12},{16,18},{18,... | collective-permute-start | bytes 393224 | tf_op jit(solution)/shard_map/ppermute | solution.py:201
  17.0 0.7 %collective-permute-start = (bf16[64,1024]{1,0:T(8,128)(2,1)S(1)}, bf16[64,1024]{1,0:T(8,128)(2,1)S(1)}, u32[]{:S(2)}, u32[]{:S(2)}) collective-permute-start(bf16[64,1024]{1,0:T(8,128)(2,1)S(1)} %get-tuple-element.24.low_ref), channel_id=1, source_target_pairs={{2,4},{4,2},{6,8},{8,6},{10,12},{12,10},{14,16},{16,14},{18,20},{2... | collective-permute-start | bytes 393224 | tf_op jit(solution)/shard_map/ppermute | solution.py:200
  17.7 4.8 %collective-permute-done.1.near_ref = bf16[64,1024]{1,0:T(8,128)(2,1)S(1)} collective-permute-done((bf16[64,1024]{1,0:T(8,128)(2,1)S(1)}, bf16[64,1024]{1,0:T(8,128)(2,1)S(1)}, u32[]{:S(2)}, u32[]{:S(2)}) %collective-permute-start.1) | collective-permute-done | bytes 131104 | tf_op jit(solution)/shard_map/ppermute | solution.py:201
  22.4 0.0 collective-permute-done.far_ref
  22.4 2.0 %shard_map.67 = (f32[64,1024]{1,0:T(8,128)S(1)}, f32[32,128]{1,0:T(8,128)S(1)}) custom-call(s32[1,128]{1,0:T(1,128)S(1)} %get-tuple-element.19.firsts_ref, bf16[64,1024]{1,0:T(8,128)(2,1)S(1)} %collective-permute-done.far_ref, bf16[64,1024]{1,0:T(8,128)(2,1)S(1)} %get-tuple-element.24.low_ref, bf16[64,1024]{1,0:T(8,128)(2,1)S(1)} %collective-permute-done.1.near_ref, ...), custom_call_target="tpu_custom_call" | custom-call | tf_op jit(solution)/shard_map/pallas_call | solution.py:202
  24.4 12.1 %all_to_all.33 = f32[32,1,128]{2,1,0:T(1,128)S(1)} all-to-all(f32[32,1,128]{2,1,0:T(1,128)S(1)} %bitcast.18), channel_id=1, replica_groups=mesh['blk'=16,'phe'=2] {'blk','phe'}, dimensions={0} | all-to-all | bytes 32768 | tf_op jit(solution)/shard_map/all_to_all | solution.py:163
  36.5 0.2 shard_map.68
  36.7 0.6 %collective-permute-start.3 = (bf16[64,1024]{1,0:T(8,128)(2,1)S(1)}, bf16[64,1024]{1,0:T(8,128)(2,1)S(1)}, u32[]{:S(2)}, u32[]{:S(2)}) collective-permute-start(bf16[64,1024]{1,0:T(8,128)(2,1)S(1)} %get-tuple-element.29.low_ref), channel_id=1, source_target_pairs={{0,2},{2,0},{4,6},{6,4},{8,10},{10,8},{12,14},{14,12},{16,18},{18,... | collective-permute-start | bytes 393224 | tf_op jit(solution)/shard_map/ppermute | solution.py:201
  37.3 0.7 %collective-permute-start.2 = (bf16[64,1024]{1,0:T(8,128)(2,1)S(1)}, bf16[64,1024]{1,0:T(8,128)(2,1)S(1)}, u32[]{:S(2)}, u32[]{:S(2)}) collective-permute-start(bf16[64,1024]{1,0:T(8,128)(2,1)S(1)} %get-tuple-element.29.low_ref), channel_id=1, source_target_pairs={{2,4},{4,2},{6,8},{8,6},{10,12},{12,10},{14,16},{16,14},{18,20},{2... | collective-permute-start | bytes 393224 | tf_op jit(solution)/shard_map/ppermute | solution.py:200
  38.0 4.8 %collective-permute-done.3.near_ref = bf16[64,1024]{1,0:T(8,128)(2,1)S(1)} collective-permute-done((bf16[64,1024]{1,0:T(8,128)(2,1)S(1)}, bf16[64,1024]{1,0:T(8,128)(2,1)S(1)}, u32[]{:S(2)}, u32[]{:S(2)}) %collective-permute-start.3) | collective-permute-done | bytes 131104 | tf_op jit(solution)/shard_map/ppermute | solution.py:201
  42.8 0.0 collective-permute-done.2.far_ref
  42.8 2.0 %shard_map.69 = (f32[64,1024]{1,0:T(8,128)S(1)}, f32[32,128]{1,0:T(8,128)S(1)}) custom-call(s32[1,128]{1,0:T(1,128)S(1)} %get-tuple-element.19.firsts_ref, bf16[64,1024]{1,0:T(8,128)(2,1)S(1)} %collective-permute-done.2.far_ref, bf16[64,1024]{1,0:T(8,128)(2,1)S(1)} %get-tuple-element.29.low_ref, bf16[64,1024]{1,0:T(8,128)(2,1)S(1)} %collective-permute-done.3.near_ref, ...), custom_call_target="tpu_custom_call" | custom-call | tf_op jit(solution)/shard_map/pallas_call | solution.py:202
  44.8 12.1 %all_to_all.34 = f32[32,1,128]{2,1,0:T(1,128)S(1)} all-to-all(f32[32,1,128]{2,1,0:T(1,128)S(1)} %bitcast.17), channel_id=1, replica_groups=mesh['blk'=16,'phe'=2] {'blk','phe'}, dimensions={0} | all-to-all | bytes 32768 | tf_op jit(solution)/shard_map/all_to_all | solution.py:163
  56.8 0.9 %shard_map.70 = f32[64,1024]{1,0:T(8,128)} custom-call(f32[32,128]{1,0:T(8,128)S(1)} %bitcast.16, s32[1,64]{1,0:T(1,128)S(1)} %bitcast.21, f32[64,1024]{1,0:T(8,128)S(1)} %get-tuple-element.32.value_ref, f32[64,1024]{1,0:T(8,128)S(1)} %get-tuple-element.22.psi_ref, bf16[3,64,1024]{2,1,0:T(8,128)(2,1)S(1)} %get-tuple-element.23.noise_ref), custom_call_target="tpu_custom_call" | custom-call | tf_op jit(solution)/shard_map/pallas_call | solution.py:186
Async XLA Ops:
  0.0 16.1 %copy-start = (s32[64]{0:T(128)S(1)}, s32[64]{0:T(128)}, u32[]{:S(2)}) copy-start(s32[64]{0:T(128)} %param.11) | copy-start | bytes 772
  1.7 14.4 %all-to-all-start = ((f32[32,1,128]{2,1,0:T(1,128)}), f32[32,1,128]{2,1,0:T(1,128)S(1)}, u32[]{:S(2)}, u32[]{:S(2)}) async-start(f32[32,1,128]{2,1,0:T(1,128)} %bitcast.2), calls=%async_computation | async-start | bytes 32768 | tf_op jit(solution)/shard_map/all_to_all | solution.py:163
  16.4 6.0 %collective-permute-start.1 = (bf16[64,1024]{1,0:T(8,128)(2,1)S(1)}, bf16[64,1024]{1,0:T(8,128)(2,1)S(1)}, u32[]{:S(2)}, u32[]{:S(2)}) collective-permute-start(bf16[64,1024]{1,0:T(8,128)(2,1)S(1)} %get-tuple-element.24.low_ref), channel_id=1, source_target_pairs={{0,2},{2,0},{4,6},{6,4},{8,10},{10,8},{12,14},{14,12},{16,18},{18,... | collective-permute-start | bytes 393224 | tf_op jit(solution)/shard_map/ppermute | solution.py:201
  17.0 5.4 %collective-permute-start = (bf16[64,1024]{1,0:T(8,128)(2,1)S(1)}, bf16[64,1024]{1,0:T(8,128)(2,1)S(1)}, u32[]{:S(2)}, u32[]{:S(2)}) collective-permute-start(bf16[64,1024]{1,0:T(8,128)(2,1)S(1)} %get-tuple-element.24.low_ref), channel_id=1, source_target_pairs={{2,4},{4,2},{6,8},{8,6},{10,12},{12,10},{14,16},{16,14},{18,20},{2... | collective-permute-start | bytes 393224 | tf_op jit(solution)/shard_map/ppermute | solution.py:200
  36.7 6.0 %collective-permute-start.3 = (bf16[64,1024]{1,0:T(8,128)(2,1)S(1)}, bf16[64,1024]{1,0:T(8,128)(2,1)S(1)}, u32[]{:S(2)}, u32[]{:S(2)}) collective-permute-start(bf16[64,1024]{1,0:T(8,128)(2,1)S(1)} %get-tuple-element.29.low_ref), channel_id=1, source_target_pairs={{0,2},{2,0},{4,6},{6,4},{8,10},{10,8},{12,14},{14,12},{16,18},{18,... | collective-permute-start | bytes 393224 | tf_op jit(solution)/shard_map/ppermute | solution.py:201
  37.3 5.4 %collective-permute-start.2 = (bf16[64,1024]{1,0:T(8,128)(2,1)S(1)}, bf16[64,1024]{1,0:T(8,128)(2,1)S(1)}, u32[]{:S(2)}, u32[]{:S(2)}) collective-permute-start(bf16[64,1024]{1,0:T(8,128)(2,1)S(1)} %get-tuple-element.29.low_ref), channel_id=1, source_target_pairs={{2,4},{4,2},{6,8},{8,6},{10,12},{12,10},{14,16},{16,14},{18,20},{2... | collective-permute-start | bytes 393224 | tf_op jit(solution)/shard_map/ppermute | solution.py:200
where the time goes:
time: 58 us; the launch traced here: 57.8 us
  blocking collectives  24.1 us (42%)
  waiting for transfers between devices  14.8 us (26%)
  starting transfers between devices  9.84 us (17%)
  Pallas kernels  8.95 us (15%)
    all_to_all x2, blocking collectives, total(): return lax.all_to_all(sums, every, 0, 0, tiled=True)  24.1 us
    ppermute x2, waiting for transfers between devices, shards(): near_low = lax.ppermute(low, 'blk', near)  9.53 us
    all_to_all x1, starting transfers between devices, total(): return lax.all_to_all(sums, every, 0, 0, tiled=True)  7.33 us
    all_to_all x1, waiting for transfers between devices, total(): return lax.all_to_all(sums, every, 0, 0, tiled=True)  5.23 us
    pallas_call x2, Pallas kernels, shards(): pl.pallas_call(functools.partial(gradient, 'blk'), in_specs=[smem] + [vme...  3.99 us
    pallas_call x1, Pallas kernels, shards(): pl.pallas_call(load, in_specs=[hbm] * 4, out_specs=[vmem] * 4, out_shape=...  1.86 us
    pallas_call x1, Pallas kernels, shards(): pl.pallas_call(first_sums, in_specs=[hbm], out_specs=[vmem] * 2, out_shap...  1.69 us
    pallas_call x3, Pallas kernels, step(): pl.pallas_call(functools.partial(update, 'phe', groups, snps), grid=(1,),...  1.41 us
  transfers between devices with their start and end apart: 5, of which 3 were waited for; matrix products, arithmetic and copies ran while one was open for 0% of the time, Pallas kernels for 3%

commit v1 on v0

--- a/solution.py
+++ b/solution.py
@@ -78,55 +78,63 @@
             low_ref[:, cut] = beta.astype(jnp.bfloat16)
 
 
-def gradient(along, firsts_ref, far_ref, low_ref, near_ref, ld_ref, beta_hat_ref, psi_ref, beta_ref, value_ref, out_ref, wide, windows):
+def turned(buffer, start, store):
+    phenos = buffer.shape[0]
+    whole = pl.multiple_of(lax.div(start, LANES) * LANES, LANES)
+    rest = start - whole
+    turn = lax.rem(LANES - rest, LANES)
+    keep = lax.broadcasted_iota(jnp.int32, (phenos, LANES), 1) < LANES - rest
+
+    def piece(at):
+        return pltpu.roll(buffer[:, pl.ds(pl.multiple_of(whole + at, LANES), LANES)].astype(jnp.float32), turn, 1)
+
+    now = piece(0)
+    for at in range(0, (buffer.shape[1] - LANES) // 3 // LANES * LANES, LANES):
+        after = piece(at + LANES)
+        store(slice(at, at + LANES), jnp.where(keep, now, after).astype(jnp.bfloat16))
+        now = after
+
+
+def product_with(low, ld_ref, cut):
+    return lax.dot_general(low, ld_ref[cut], (((1,), (1,)), ((), ())), preferred_element_type=jnp.float32)
+
+
+def inner(along, firsts_ref, low_ref, ld_ref, beta_hat_ref, psi_ref, beta_ref, grad_ref, scale_ref, wide, windows, slots):
     rows, span = ld_ref.shape
     phenos = low_ref.shape[0]
-    place = lax.axis_index(along)
-    base = place * rows
-    odd = lax.rem(place, 2)
+    base = lax.axis_index(along) * rows
     tiles = rows // TILE
     steps = 2 * TILE // LANES
-    for third, part in ((0, far_ref), (1, low_ref), (2, near_ref)):
-        at = pl.multiple_of(jnp.where(odd == 1, 2 - third, third) * span, LANES)
-        wide[:, pl.ds(at, span)] = part[...]
-    lane = lax.broadcasted_iota(jnp.int32, (phenos, LANES), 1)
+    wide[...] = jnp.zeros_like(wide)
+    wide[:, span : 2 * span] = low_ref[...]
 
     def fill(slot, first):
-        start = first - base + span
-        whole = pl.multiple_of(lax.div(start, LANES) * LANES, LANES)
-        rest = start - whole
-        turn = lax.rem(LANES - rest, LANES)
-        keep = lane < LANES - rest
-        now = pltpu.roll(wide[:, pl.ds(whole, LANES)].astype(jnp.float32), turn, 1)
-        for at in range(0, span, LANES):
-            after = pltpu.roll(wide[:, pl.ds(pl.multiple_of(whole + at + LANES, LANES), LANES)].astype(jnp.float32), turn, 1)
-            windows[slot, :, at : at + LANES] = jnp.where(keep, now, after).astype(jnp.bfloat16)
-            now = after
-
-    slot = 0
-    before = firsts_ref[0, 0]
-    fill(0, before)
-    slots = []
-    for number in range(tiles * steps):
-        if number:
-            first = firsts_ref[0, number]
-            fresh = first != before
-            slot = slot + fresh.astype(jnp.int32)
-
-            @pl.when(fresh)
-            def _(slot=slot, first=first):
-                fill(slot, first)
-
-            before = first
-        slots.append((slot, before - base))
-
-    resid = jnp.zeros((phenos, LANES), jnp.float32)
+        def store(cut, values):
+            windows[slot, :, cut] = values
+
+        turned(wide, first - base + span, store)
+
+    fill(0, firsts_ref[0, 0])
+    slots[0] = 0
+
+    def look(number, slot):
+        first = firsts_ref[0, number]
+        fresh = first != firsts_ref[0, number - 1]
+        slot = slot + fresh.astype(jnp.int32)
+        slots[number] = slot
+
+        @pl.when(fresh)
+        def _():
+            fill(slot, first)
+
+        return slot
+
+    lax.fori_loop(1, tiles * steps, look, jnp.int32(0))
     scale = jnp.zeros((phenos, LANES), jnp.float32)
     for tile in range(tiles):
         cut = slice(tile * TILE, (tile + 1) * TILE)
-        known = slots[tile * steps : (tile + 1) * steps]
-        low = windows[pl.ds(known[0][0], WINDOWS)].reshape(WINDOWS * phenos, span)
-        product = lax.dot_general(low, ld_ref[cut], (((1,), (1,)), ((), ())), preferred_element_type=jnp.float32)
+        known = [(slots[number], firsts_ref[0, number] - base) for number in range(tile * steps, (tile + 1) * steps)]
+        product = product_with(windows[pl.ds(known[0][0], WINDOWS)].reshape(WINDOWS * phenos, span), ld_ref, cut)
         row = lax.broadcasted_iota(jnp.int32, (phenos, TILE), 1) + tile * TILE
         applied = product[:phenos]
         for turn in range(1, WINDOWS):
@@ -134,12 +142,48 @@
             for other, where in reversed(known[1:]):
                 begin = jnp.where(other == known[0][0] + turn, where, begin)
             applied = jnp.where(row >= begin, product[turn * phenos : (turn + 1) * phenos], applied)
-        grad = beta_hat_ref[:, cut] - applied
+        grad_ref[:, cut] = beta_hat_ref[:, cut] - applied
         beta = beta_ref[:, cut]
-        value_ref[:, cut] = beta + grad
+        scale = scale + chunk_sums(beta * beta / psi_ref[:, cut])
+    scale_ref[...] = scale
+
+
+def outer(along, firsts_ref, far_ref, near_ref, ld_ref, grad_ref, scale_ref, beta_ref, value_ref, out_ref, sides, windows):
+    rows, span = ld_ref.shape
+    phenos = far_ref.shape[0]
+    place = lax.axis_index(along)
+    base = place * rows
+    odd = lax.rem(place, 2) == 1
+    gap = span + LANES
+    sides[:, span : span + gap] = jnp.zeros((phenos, gap), sides.dtype)
+    sides[:, pl.ds(pl.multiple_of(jnp.where(odd, span + gap, 0), LANES), span)] = far_ref[...]
+    sides[:, pl.ds(pl.multiple_of(jnp.where(odd, 0, span + gap), LANES), span)] = near_ref[...]
+    table = firsts_ref[...]
+    count = 2 * rows // LANES
+    first = table[0, 0] - base
+    last = table[0, count - 1] - base
+    lane = lax.broadcasted_iota(jnp.int32, table.shape, 1)
+    ends = jnp.where((lane < count) & (table - base != first), table - base, rows)
+    end = jnp.min(ends.astype(jnp.float32), axis=1, keepdims=True).astype(jnp.int32)
+
+    def store_at(begin):
+        def store(cut, values):
+            windows[begin : begin + phenos, cut] = values
+
+        return store
+
+    turned(sides, first + span, store_at(0))
+    turned(sides, jnp.maximum(last, 0) + gap, store_at(phenos))
+    resid = jnp.zeros((phenos, LANES), jnp.float32)
+    for tile in range(rows // TILE):
+        cut = slice(tile * TILE, (tile + 1) * TILE)
+        product = product_with(windows[...], ld_ref, cut)
+        row = lax.broadcasted_iota(jnp.int32, (phenos, TILE), 1) + tile * TILE
+        applied = jnp.where(row < end, product[:phenos], 0.0) + jnp.where(row >= last, product[phenos:], 0.0)
+        grad = grad_ref[:, cut] - applied
+        value_ref[:, cut] = beta_ref[:, cut] + grad
         resid = resid + chunk_sums(grad * grad)
-        scale = scale + chunk_sums(beta * beta / psi_ref[:, cut])
-    spread(resid, scale, out_ref)
+    spread(resid, scale_ref[...], out_ref)
 
 
 def shards(ld_rows, block_first, beta_hat, psi, noise, sample_size):
@@ -199,17 +243,30 @@
         beta, low = step(t, sums, value)
         far_low = lax.ppermute(low, "blk", far)
         near_low = lax.ppermute(low, "blk", near)
+        grad, scale = pl.pallas_call(
+            functools.partial(inner, "blk"),
+            in_specs=[smem] + [vmem] * 5,
+            out_specs=[vmem] * 2,
+            out_shape=[wide_shape, pltpu.VMEM((phenos, LANES), jnp.float32)],
+            scratch_shapes=[
+                pltpu.VMEM((phenos, 3 * span + LANES), jnp.bfloat16),
+                pltpu.VMEM((2 * rows // LANES + WINDOWS, phenos, span), jnp.bfloat16),
+                pltpu.SMEM((2 * rows // LANES,), jnp.int32),
+            ],
+            compiler_params=params,
+            cost_estimate=pl.CostEstimate(flops=2 * WINDOWS * phenos * rows * span, bytes_accessed=4 << 20, transcendentals=0),
+        )(firsts, low, ld_rows, beta_hat, psi, beta)
         value, sums = pl.pallas_call(
-            functools.partial(gradient, "blk"),
-            in_specs=[smem] + [vmem] * 7,
+            functools.partial(outer, "blk"),
+            in_specs=[vmem] * 7,
             out_specs=[vmem] * 2,
             out_shape=[wide_shape, sums_shape],
             scratch_shapes=[
-                pltpu.VMEM((phenos, 3 * span), jnp.bfloat16),
-                pltpu.VMEM((2 * rows // LANES + WINDOWS, phenos, span), jnp.bfloat16),
+                pltpu.VMEM((phenos, 3 * span + LANES), jnp.bfloat16),
+                pltpu.VMEM((2 * phenos, span), jnp.bfloat16),
             ],
             compiler_params=params,
-        )(firsts, far_low, low, near_low, ld_rows, beta_hat, psi, beta)
+        )(firsts, far_low, near_low, ld_rows, grad, scale, beta)
         sums = total(sums)
     return step(ITERS - 1, sums, value)
 

time: 58 us -> 56.1 us (0.967)
  waiting for transfers between devices: 14.8 us -> 10.8 us
  Pallas kernels: 8.95 us -> 11 us
    ppermute x2, waiting for transfers between devices: 9.53 us -> 5.57 us  [shards(): near_low = lax.ppermute(low, 'blk', near)]
    pallas_call x2 -> x4, Pallas kernels: 3.99 us -> 6.04 us  [the longest x2 3.95 us: shards(): pl.pallas_call(functools.partial(inner, 'blk'), in_specs=[smem] + [vmem]...]
  transfers between devices with their start and end apart: 5 -> 5, of which waited for: 3 -> 3; matrix products, arithmetic and copies ran while one was open for 0% -> 0% of each run, Pallas kernels for 3% -> 10%
where the time goes in v1:
time: 56.1 us; the launch traced here: 55.9 us
  blocking collectives  24.1 us (43%)
  Pallas kernels  11 us (20%)
  waiting for transfers between devices  10.8 us (19%)
  starting transfers between devices  9.84 us (18%)
    all_to_all x2, blocking collectives, total(): return lax.all_to_all(sums, every, 0, 0, tiled=True)  24.1 us
    all_to_all x1, starting transfers between devices, total(): return lax.all_to_all(sums, every, 0, 0, tiled=True)  7.33 us
    ppermute x2, waiting for transfers between devices, shards(): near_low = lax.ppermute(low, 'blk', near)  5.57 us
    all_to_all x1, waiting for transfers between devices, total(): return lax.all_to_all(sums, every, 0, 0, tiled=True)  5.23 us
    pallas_call x2, Pallas kernels, shards(): pl.pallas_call(functools.partial(inner, 'blk'), in_specs=[smem] + [vmem]...  3.95 us
    pallas_call x2, Pallas kernels, shards(): pl.pallas_call(functools.partial(outer, 'blk'), in_specs=[vmem] * 7, out_...  2.08 us
    pallas_call x1, Pallas kernels, shards(): pl.pallas_call(load, in_specs=[hbm] * 4, out_specs=[vmem] * 4, out_shape=...  1.86 us
    pallas_call x1, Pallas kernels, shards(): pl.pallas_call(first_sums, in_specs=[hbm], out_specs=[vmem] * 2, out_shap...  1.69 us
  transfers between devices with their start and end apart: 5, of which 3 were waited for; matrix products, arithmetic and copies ran while one was open for 0% of the time, Pallas kernels for 10%

profile of v1, /device:TPU:0, one launch (start us, length us, event | category | flops | bytes accessed | tf_op | source)
XLA Modules:
  0.0 55.9 jit_solution(3491748300935580246)
XLA Ops:
  0.0 0.0 copy-start
  0.0 1.7 %shard_map.65 = (f32[64,1024]{1,0:T(8,128)S(1)}, f32[32,128]{1,0:T(8,128)}) custom-call(f32[64,1024]{1,0:T(8,128)} %beta_hat_ref.1), custom_call_target="tpu_custom_call" | custom-call | tf_op jit(solution)/shard_map/pallas_call | solution.py:209
  1.7 7.3 %all-to-all-start = ((f32[32,1,128]{2,1,0:T(1,128)}), f32[32,1,128]{2,1,0:T(1,128)S(1)}, u32[]{:S(2)}, u32[]{:S(2)}) async-start(f32[32,1,128]{2,1,0:T(1,128)} %bitcast.2), calls=%async_computation | async-start | bytes 32768 | tf_op jit(solution)/shard_map/all_to_all | solution.py:207
  9.0 1.9 %shard_map.64 = (f32[64,1024]{1,0:T(8,128)S(1)}, bf16[3,64,1024]{2,1,0:T(8,128)(2,1)S(1)}, bf16[1024,1024]{1,0:T(8,128)(2,1)S(1)}, s32[1,128]{1,0:T(1,128)S(1)}) custom-call(s32[8,128]{1,0:T(8,128)} %bitcast.22, f32[64,1024]{1,0:T(8,128)} %psi_ref.1, bf16[3,64,1024]{2,1,0:T(8,128)(2,1)} %noise_ref.1, bf16[1024,1024]{1,0:T(8,128)(2,1)} %ld_ref.1), custom_call_target="tpu_custom_call" | custom-call | flops 16777216 | bytes 3145728 | tf_op jit(solution)/shard_map/pallas_call | solution.py:218
  10.9 5.2 %all-to-all-done = f32[32,1,128]{2,1,0:T(1,128)S(1)} async-done(((f32[32,1,128]{2,1,0:T(1,128)}), f32[32,1,128]{2,1,0:T(1,128)S(1)}, u32[]{:S(2)}, u32[]{:S(2)}) %all-to-all-start) | async-done | bytes 16416 | tf_op jit(solution)/shard_map/all_to_all | solution.py:207
  16.1 0.0 copy-done
  16.1 0.2 shard_map.66
  16.4 0.6 %collective-permute-start.1 = (bf16[64,1024]{1,0:T(8,128)(2,1)S(1)}, bf16[64,1024]{1,0:T(8,128)(2,1)S(1)}, u32[]{:S(2)}, u32[]{:S(2)}) collective-permute-start(bf16[64,1024]{1,0:T(8,128)(2,1)S(1)} %get-tuple-element.28.low_ref), channel_id=1, source_target_pairs={{0,2},{2,0},{4,6},{6,4},{8,10},{10,8},{12,14},{14,12},{16,18},{18,... | collective-permute-start | bytes 393224 | tf_op jit(solution)/shard_map/ppermute | solution.py:245
  17.0 0.7 %collective-permute-start = (bf16[64,1024]{1,0:T(8,128)(2,1)S(1)}, bf16[64,1024]{1,0:T(8,128)(2,1)S(1)}, u32[]{:S(2)}, u32[]{:S(2)}) collective-permute-start(bf16[64,1024]{1,0:T(8,128)(2,1)S(1)} %get-tuple-element.28.low_ref), channel_id=1, source_target_pairs={{2,4},{4,2},{6,8},{8,6},{10,12},{12,10},{14,16},{16,14},{18,20},{2... | collective-permute-start | bytes 393224 | tf_op jit(solution)/shard_map/ppermute | solution.py:244
  17.7 2.0 %shard_map.67 = (f32[64,1024]{1,0:T(8,128)S(1)}, f32[64,128]{1,0:T(8,128)S(1)}) custom-call(s32[1,128]{1,0:T(1,128)S(1)} %get-tuple-element.23.firsts_ref, bf16[64,1024]{1,0:T(8,128)(2,1)S(1)} %get-tuple-element.28.low_ref, bf16[1024,1024]{1,0:T(8,128)(2,1)S(1)} %get-tuple-element.29.ld_ref, f32[64,1024]{1,0:T(8,128)S(1)} %get-tuple-element.25.value_ref.beta_hat_ref, ...), custom_call_target="tpu_custom_call" | custom-call | flops 402653184 | bytes 4194304 | tf_op jit(solution)/shard_map/pallas_call | solution.py:246
  19.6 2.8 %collective-permute-done.1.near_ref = bf16[64,1024]{1,0:T(8,128)(2,1)S(1)} collective-permute-done((bf16[64,1024]{1,0:T(8,128)(2,1)S(1)}, bf16[64,1024]{1,0:T(8,128)(2,1)S(1)}, u32[]{:S(2)}, u32[]{:S(2)}) %collective-permute-start.1) | collective-permute-done | bytes 131104 | tf_op jit(solution)/shard_map/ppermute | solution.py:245
  22.4 0.0 collective-permute-done.far_ref
  22.4 1.0 %shard_map.68 = (f32[64,1024]{1,0:T(8,128)S(1)}, f32[32,128]{1,0:T(8,128)S(1)}) custom-call(s32[1,128]{1,0:T(1,128)S(1)} %get-tuple-element.23.firsts_ref, bf16[64,1024]{1,0:T(8,128)(2,1)S(1)} %collective-permute-done.far_ref, bf16[64,1024]{1,0:T(8,128)(2,1)S(1)} %collective-permute-done.1.near_ref, bf16[1024,1024]{1,0:T(8,128)(2,1)S(1)} %get-tuple-element.29.ld_ref, ...), custom_call_target="tpu_custom_call" | custom-call | tf_op jit(solution)/shard_map/pallas_call | solution.py:259
  23.5 12.1 %all_to_all.33 = f32[32,1,128]{2,1,0:T(1,128)S(1)} all-to-all(f32[32,1,128]{2,1,0:T(1,128)S(1)} %bitcast.18), channel_id=1, replica_groups=mesh['blk'=16,'phe'=2] {'blk','phe'}, dimensions={0} | all-to-all | bytes 32768 | tf_op jit(solution)/shard_map/all_to_all | solution.py:207
  35.5 0.2 shard_map.69
  35.8 0.6 %collective-permute-start.3 = (bf16[64,1024]{1,0:T(8,128)(2,1)S(1)}, bf16[64,1024]{1,0:T(8,128)(2,1)S(1)}, u32[]{:S(2)}, u32[]{:S(2)}) collective-permute-start(bf16[64,1024]{1,0:T(8,128)(2,1)S(1)} %get-tuple-element.35.low_ref), channel_id=1, source_target_pairs={{0,2},{2,0},{4,6},{6,4},{8,10},{10,8},{12,14},{14,12},{16,18},{18,... | collective-permute-start | bytes 393224 | tf_op jit(solution)/shard_map/ppermute | solution.py:245
  36.4 0.7 %collective-permute-start.2 = (bf16[64,1024]{1,0:T(8,128)(2,1)S(1)}, bf16[64,1024]{1,0:T(8,128)(2,1)S(1)}, u32[]{:S(2)}, u32[]{:S(2)}) collective-permute-start(bf16[64,1024]{1,0:T(8,128)(2,1)S(1)} %get-tuple-element.35.low_ref), channel_id=1, source_target_pairs={{2,4},{4,2},{6,8},{8,6},{10,12},{12,10},{14,16},{16,14},{18,20},{2... | collective-permute-start | bytes 393224 | tf_op jit(solution)/shard_map/ppermute | solution.py:244
  37.0 2.0 %shard_map.70 = (f32[64,1024]{1,0:T(8,128)S(1)}, f32[64,128]{1,0:T(8,128)S(1)}) custom-call(s32[1,128]{1,0:T(1,128)S(1)} %get-tuple-element.23.firsts_ref, bf16[64,1024]{1,0:T(8,128)(2,1)S(1)} %get-tuple-element.35.low_ref, bf16[1024,1024]{1,0:T(8,128)(2,1)S(1)} %get-tuple-element.29.ld_ref, f32[64,1024]{1,0:T(8,128)S(1)} %get-tuple-element.25.value_ref.beta_hat_ref, ...), custom_call_target="tpu_custom_call" | custom-call | flops 402653184 | bytes 4194304 | tf_op jit(solution)/shard_map/pallas_call | solution.py:246
  39.0 2.8 %collective-permute-done.3.near_ref = bf16[64,1024]{1,0:T(8,128)(2,1)S(1)} collective-permute-done((bf16[64,1024]{1,0:T(8,128)(2,1)S(1)}, bf16[64,1024]{1,0:T(8,128)(2,1)S(1)}, u32[]{:S(2)}, u32[]{:S(2)}) %collective-permute-start.3) | collective-permute-done | bytes 131104 | tf_op jit(solution)/shard_map/ppermute | solution.py:245
  41.8 0.0 collective-permute-done.2.far_ref
  41.8 1.0 %shard_map.71 = (f32[64,1024]{1,0:T(8,128)S(1)}, f32[32,128]{1,0:T(8,128)S(1)}) custom-call(s32[1,128]{1,0:T(1,128)S(1)} %get-tuple-element.23.firsts_ref, bf16[64,1024]{1,0:T(8,128)(2,1)S(1)} %collective-permute-done.2.far_ref, bf16[64,1024]{1,0:T(8,128)(2,1)S(1)} %collective-permute-done.3.near_ref, bf16[1024,1024]{1,0:T(8,128)(2,1)S(1)} %get-tuple-element.29.ld_ref, ...), custom_call_target="tpu_custom_call" | custom-call | tf_op jit(solution)/shard_map/pallas_call | solution.py:259
  42.9 12.1 %all_to_all.34 = f32[32,1,128]{2,1,0:T(1,128)S(1)} all-to-all(f32[32,1,128]{2,1,0:T(1,128)S(1)} %bitcast.17), channel_id=1, replica_groups=mesh['blk'=16,'phe'=2] {'blk','phe'}, dimensions={0} | all-to-all | bytes 32768 | tf_op jit(solution)/shard_map/all_to_all | solution.py:207
  54.9 0.9 %shard_map.72 = f32[64,1024]{1,0:T(8,128)} custom-call(f32[32,128]{1,0:T(8,128)S(1)} %bitcast.16, s32[1,64]{1,0:T(1,128)S(1)} %bitcast.21, f32[64,1024]{1,0:T(8,128)S(1)} %get-tuple-element.40.value_ref, f32[64,1024]{1,0:T(8,128)S(1)} %get-tuple-element.26.psi_ref, bf16[3,64,1024]{2,1,0:T(8,128)(2,1)S(1)} %get-tuple-element.27.noise_ref), custom_call_target="tpu_custom_call" | custom-call | tf_op jit(solution)/shard_map/pallas_call | solution.py:230
Async XLA Ops:
  0.0 16.1 %copy-start = (s32[64]{0:T(128)S(1)}, s32[64]{0:T(128)}, u32[]{:S(2)}) copy-start(s32[64]{0:T(128)} %param.11) | copy-start | bytes 772
  1.7 14.4 %all-to-all-start = ((f32[32,1,128]{2,1,0:T(1,128)}), f32[32,1,128]{2,1,0:T(1,128)S(1)}, u32[]{:S(2)}, u32[]{:S(2)}) async-start(f32[32,1,128]{2,1,0:T(1,128)} %bitcast.2), calls=%async_computation | async-start | bytes 32768 | tf_op jit(solution)/shard_map/all_to_all | solution.py:207
  16.4 6.0 %collective-permute-start.1 = (bf16[64,1024]{1,0:T(8,128)(2,1)S(1)}, bf16[64,1024]{1,0:T(8,128)(2,1)S(1)}, u32[]{:S(2)}, u32[]{:S(2)}) collective-permute-start(bf16[64,1024]{1,0:T(8,128)(2,1)S(1)} %get-tuple-element.28.low_ref), channel_id=1, source_target_pairs={{0,2},{2,0},{4,6},{6,4},{8,10},{10,8},{12,14},{14,12},{16,18},{18,... | collective-permute-start | bytes 393224 | tf_op jit(solution)/shard_map/ppermute | solution.py:245
  17.0 5.4 %collective-permute-start = (bf16[64,1024]{1,0:T(8,128)(2,1)S(1)}, bf16[64,1024]{1,0:T(8,128)(2,1)S(1)}, u32[]{:S(2)}, u32[]{:S(2)}) collective-permute-start(bf16[64,1024]{1,0:T(8,128)(2,1)S(1)} %get-tuple-element.28.low_ref), channel_id=1, source_target_pairs={{2,4},{4,2},{6,8},{8,6},{10,12},{12,10},{14,16},{16,14},{18,20},{2... | collective-permute-start | bytes 393224 | tf_op jit(solution)/shard_map/ppermute | solution.py:244
  35.8 6.0 %collective-permute-start.3 = (bf16[64,1024]{1,0:T(8,128)(2,1)S(1)}, bf16[64,1024]{1,0:T(8,128)(2,1)S(1)}, u32[]{:S(2)}, u32[]{:S(2)}) collective-permute-start(bf16[64,1024]{1,0:T(8,128)(2,1)S(1)} %get-tuple-element.35.low_ref), channel_id=1, source_target_pairs={{0,2},{2,0},{4,6},{6,4},{8,10},{10,8},{12,14},{14,12},{16,18},{18,... | collective-permute-start | bytes 393224 | tf_op jit(solution)/shard_map/ppermute | solution.py:245
  36.4 5.4 %collective-permute-start.2 = (bf16[64,1024]{1,0:T(8,128)(2,1)S(1)}, bf16[64,1024]{1,0:T(8,128)(2,1)S(1)}, u32[]{:S(2)}, u32[]{:S(2)}) collective-permute-start(bf16[64,1024]{1,0:T(8,128)(2,1)S(1)} %get-tuple-element.35.low_ref), channel_id=1, source_target_pairs={{2,4},{4,2},{6,8},{8,6},{10,12},{12,10},{14,16},{16,14},{18,20},{2... | collective-permute-start | bytes 393224 | tf_op jit(solution)/shard_map/ppermute | solution.py:244

commit v2 on v1

--- a/solution.py
+++ b/solution.py
@@ -30,16 +30,20 @@
     out_ref[...] = jnp.broadcast_to(row, out_ref.shape)
 
 
-def first_sums(beta_hat_ref, kept_ref, out_ref, sem):
-    copy = pltpu.make_async_copy(beta_hat_ref, kept_ref, sem)
-    copy.start()
-    copy.wait()
-    grad = kept_ref[...]
+def begin(beta_hat_ref, psi_ref, noise_ref, size_ref, beta_hat_out, psi_out, noise_out, size_out, out_ref, sems):
+    pairs = (beta_hat_ref, beta_hat_out), (psi_ref, psi_out), (noise_ref, noise_out), (size_ref, size_out)
+    copies = [pltpu.make_async_copy(a, b, sems.at[n]) for n, (a, b) in enumerate(pairs)]
+    for copy in copies:
+        copy.start()
+    copies[0].wait()
+    grad = beta_hat_out[...]
     spread(grad * grad, jnp.zeros_like(grad), out_ref)
-
-
-def load(block_first_ref, psi_ref, noise_ref, ld_ref, psi_out, noise_out, ld_out, table_ref, starts, sems):
-    pairs = (block_first_ref, starts), (psi_ref, psi_out), (noise_ref, noise_out), (ld_ref, ld_out)
+    for copy in copies[1:]:
+        copy.wait()
+
+
+def load(after_ref, block_first_ref, ld_ref, ld_out, table_ref, starts, sems):
+    pairs = (block_first_ref, starts), (ld_ref, ld_out)
     copies = [pltpu.make_async_copy(a, b, sems.at[n]) for n, (a, b) in enumerate(pairs)]
     for copy in copies:
         copy.start()
@@ -50,11 +54,10 @@
     start = jnp.where(lane == row, jnp.broadcast_to(first[:, :1], first.shape), 0)
     end = jnp.where(lane == row + 1, jnp.broadcast_to(first[:, LANES - 1 :], first.shape), 0)
     table_ref[...] = jnp.sum(start + end, axis=0, keepdims=True)
-    for copy in copies[1:]:
-        copy.wait()
-
-
-def update(own, groups, snps, sums_ref, sample_size_ref, value_ref, psi_ref, noise_ref, beta_ref, low_ref=None):
+    copies[1].wait()
+
+
+def update(own, groups, snps, t, sums_ref, sample_size_ref, value_ref, psi_ref, noise_ref, beta_ref, low_ref=None):
     sums = sums_ref[...]
     half = sums.shape[1] // 2
     member = lax.rem(lax.broadcasted_iota(jnp.int32, sums.shape, 0), groups) == lax.axis_index(own)
@@ -72,7 +75,7 @@
     for at in range(0, psi_ref.shape[1], LANES):
         cut = slice(at, at + LANES)
         psi = psi_ref[:, cut]
-        beta = psi / (psi + phi) * (value_ref[:, cut] + amp * noise_ref[0, :, cut].astype(jnp.float32))
+        beta = psi / (psi + phi) * (value_ref[:, cut] + amp * noise_ref[t, :, cut].astype(jnp.float32))
         beta_ref[:, cut] = beta
         if low_ref is not None:
             low_ref[:, cut] = beta.astype(jnp.bfloat16)
@@ -206,35 +209,31 @@
     def total(sums):
         return lax.all_to_all(sums, every, 0, 0, tiled=True)
 
-    beta_hat, sums = pl.pallas_call(
-        first_sums,
-        in_specs=[hbm],
-        out_specs=[vmem] * 2,
-        out_shape=[wide_shape, sums_shape],
-        scratch_shapes=[pltpu.SemaphoreType.DMA],
+    beta_hat, psi, noise, sample_size, sums = pl.pallas_call(
+        begin,
+        in_specs=[hbm] * 4,
+        out_specs=[vmem] * 5,
+        out_shape=[
+            wide_shape,
+            wide_shape,
+            pltpu.VMEM(noise.shape, noise.dtype),
+            pltpu.VMEM((1, phenos), jnp.int32),
+            sums_shape,
+        ],
+        scratch_shapes=[pltpu.SemaphoreType.DMA((4,))],
         compiler_params=params,
-    )(here(beta_hat))
+    )(*map(here, (beta_hat, psi, noise, sample_size[None])))
     sums = total(sums)
-    psi, noise, ld_rows, firsts = pl.pallas_call(
-        load,
-        in_specs=[hbm] * 4,
-        out_specs=[vmem] * 4,
-        out_shape=[wide_shape, pltpu.VMEM(noise.shape, noise.dtype), pltpu.VMEM(ld_rows.shape, ld_rows.dtype), pltpu.VMEM((1, LANES), jnp.int32)],
-        scratch_shapes=[pltpu.VMEM((rows // LANES, LANES), jnp.int32), pltpu.SemaphoreType.DMA((4,))],
-        compiler_params=params,
-        cost_estimate=pl.CostEstimate(flops=1 << 24, bytes_accessed=3 << 20, transcendentals=0),
-    )(*map(here, (block_first.reshape(-1, LANES), psi, noise, ld_rows)))
 
     def step(t, sums, value):
         last = t == ITERS - 1
         return pl.pallas_call(
-            functools.partial(update, "phe", groups, snps),
-            grid=(1,),
-            in_specs=[vmem] * 4 + [pl.BlockSpec((1,) + beta_hat.shape, lambda i: (t, 0, 0))],
+            functools.partial(update, "phe", groups, snps, t),
+            in_specs=[vmem] * 5,
             out_specs=vmem if last else [vmem] * 2,
             out_shape=jax.ShapeDtypeStruct(beta_hat.shape, jnp.float32) if last else [wide_shape, low_shape],
             compiler_params=params,
-        )(sums, sample_size[None], value, psi, noise)
+        )(sums, sample_size, value, psi, noise)
 
     far = [(i, i + 1 if i % 2 else i - 1) for i in range(1, blocks - 1 + blocks % 2)]
     near = [(i, i ^ 1) for i in range(blocks - blocks % 2)]
@@ -243,6 +242,16 @@
         beta, low = step(t, sums, value)
         far_low = lax.ppermute(low, "blk", far)
         near_low = lax.ppermute(low, "blk", near)
+        if t == 0:
+            ld_rows, firsts = pl.pallas_call(
+                load,
+                in_specs=[vmem] + [hbm] * 2,
+                out_specs=[vmem] * 2,
+                out_shape=[pltpu.VMEM(ld_rows.shape, ld_rows.dtype), pltpu.VMEM((1, LANES), jnp.int32)],
+                scratch_shapes=[pltpu.VMEM((rows // LANES, LANES), jnp.int32), pltpu.SemaphoreType.DMA((2,))],
+                compiler_params=params,
+                cost_estimate=pl.CostEstimate(flops=1 << 26, bytes_accessed=3 << 20, transcendentals=0),
+            )(low, here(block_first.reshape(-1, LANES)), here(ld_rows))
         grad, scale = pl.pallas_call(
             functools.partial(inner, "blk"),
             in_specs=[smem] + [vmem] * 5,

time: 56.1 us -> 55.5 us (0.989)
  blocking collectives: 24.1 us -> 38.4 us
  starting transfers between devices: 9.84 us -> 2.51 us
  waiting for transfers between devices: 10.8 us -> 3.95 us
  Pallas kernels: 11 us -> 10.3 us
    all_to_all x2 -> x3, blocking collectives: 24.1 us -> 38.4 us  [total(): return lax.all_to_all(sums, every, 0, 0, tiled=True)]
    all_to_all x1 -> x0, starting transfers between devices: 7.33 us -> none  [total(): return lax.all_to_all(sums, every, 0, 0, tiled=True)]
    all_to_all x1 -> x0, waiting for transfers between devices: 5.23 us -> none  [total(): return lax.all_to_all(sums, every, 0, 0, tiled=True)]
    ppermute x2, waiting for transfers between devices: 5.57 us -> 3.95 us  [shards(): near_low = lax.ppermute(low, 'blk', near)]
    pallas_call x5, Pallas kernels: 4.97 us -> 4.23 us  [the longest x1 1.63 us: shards(): pl.pallas_call(load, in_specs=[vmem] + [hbm] * 2, out_specs=[vmem] * 2, o...]
  transfers between devices with their start and end apart: 5 -> 4, of which waited for: 3 -> 2; matrix products, arithmetic and copies ran while one was open for 0% -> 0% of each run, Pallas kernels for 10% -> 10%
where the time goes in v2:
time: 55.5 us; the launch traced here: 55.2 us
  blocking collectives  38.4 us (69%)
  Pallas kernels  10.3 us (19%)
  waiting for transfers between devices  3.95 us (7%)
  starting transfers between devices  2.51 us (5%)
    all_to_all x3, blocking collectives, total(): return lax.all_to_all(sums, every, 0, 0, tiled=True)  38.4 us
    ppermute x2, waiting for transfers between devices, shards(): near_low = lax.ppermute(low, 'blk', near)  3.95 us
    pallas_call x2, Pallas kernels, shards(): pl.pallas_call(functools.partial(inner, 'blk'), in_specs=[smem] + [vmem]...  3.93 us
    pallas_call x2, Pallas kernels, shards(): pl.pallas_call(functools.partial(outer, 'blk'), in_specs=[vmem] * 7, out_...  2.09 us
    pallas_call x1, Pallas kernels, shards(): pl.pallas_call(load, in_specs=[vmem] + [hbm] * 2, out_specs=[vmem] * 2, o...  1.63 us
    pallas_call x3, Pallas kernels, step(): pl.pallas_call(functools.partial(update, 'phe', groups, snps, t), in_spec...  1.42 us
    ppermute x2, starting transfers between devices, shards(): far_low = lax.ppermute(low, 'blk', far)  1.31 us
    ppermute x2, starting transfers between devices, shards(): near_low = lax.ppermute(low, 'blk', near)  1.19 us
  transfers between devices with their start and end apart: 4, of which 2 were waited for; matrix products, arithmetic and copies ran while one was open for 0% of the time, Pallas kernels for 10%

profile of v2, /device:TPU:0, one launch (start us, length us, event | category | flops | bytes accessed | tf_op | source)
XLA Modules:
  0.0 55.2 jit_solution(16040659152160846824)
XLA Ops:
  0.0 1.2 %shard_map.64 = (f32[64,1024]{1,0:T(8,128)S(1)}, f32[64,1024]{1,0:T(8,128)S(1)}, bf16[3,64,1024]{2,1,0:T(8,128)(2,1)S(1)}, s32[1,64]{1,0:T(1,128)S(1)}, f32[32,128]{1,0:T(8,128)S(1)}) custom-call(f32[64,1024]{1,0:T(8,128)} %beta_hat_ref.1, f32[64,1024]{1,0:T(8,128)} %psi_ref.1, bf16[3,64,1024]{2,1,0:T(8,128)(2,1)} %noise_ref.1, s32[1,64]{1,0:T(1,128)} %bitcast.21), custom_call_target="tpu_custom_call" | custom-call | tf_op jit(solution)/shard_map/pallas_call | solution.py:212
  1.2 14.3 %all_to_all.33 = f32[32,1,128]{2,1,0:T(1,128)S(1)} all-to-all(f32[32,1,128]{2,1,0:T(1,128)S(1)} %bitcast.19), channel_id=1, replica_groups=mesh['blk'=16,'phe'=2] {'blk','phe'}, dimensions={0} | all-to-all | bytes 32768 | tf_op jit(solution)/shard_map/all_to_all | solution.py:210
  15.5 0.2 shard_map.65
  15.8 0.6 %collective-permute-start.1 = (bf16[64,1024]{1,0:T(8,128)(2,1)S(1)}, bf16[64,1024]{1,0:T(8,128)(2,1)S(1)}, u32[]{:S(2)}, u32[]{:S(2)}) collective-permute-start(bf16[64,1024]{1,0:T(8,128)(2,1)S(1)} %get-tuple-element.29.after_ref.low_ref), channel_id=1, source_target_pairs={{0,2},{2,0},{4,6},{6,4},{8,10},{10,8},{12,14},{14,12},{16,18},{18,... | collective-permute-start | bytes 393224 | tf_op jit(solution)/shard_map/ppermute | solution.py:244
  16.4 0.7 %collective-permute-start = (bf16[64,1024]{1,0:T(8,128)(2,1)S(1)}, bf16[64,1024]{1,0:T(8,128)(2,1)S(1)}, u32[]{:S(2)}, u32[]{:S(2)}) collective-permute-start(bf16[64,1024]{1,0:T(8,128)(2,1)S(1)} %get-tuple-element.29.after_ref.low_ref), channel_id=1, source_target_pairs={{2,4},{4,2},{6,8},{8,6},{10,12},{12,10},{14,16},{16,14},{18,20},{2... | collective-permute-start | bytes 393224 | tf_op jit(solution)/shard_map/ppermute | solution.py:243
  17.0 1.6 %shard_map.66 = (bf16[1024,1024]{1,0:T(8,128)(2,1)S(1)}, s32[1,128]{1,0:T(1,128)S(1)}) custom-call(bf16[64,1024]{1,0:T(8,128)(2,1)S(1)} %get-tuple-element.29.after_ref.low_ref, s32[8,128]{1,0:T(8,128)} %bitcast.20, bf16[1024,1024]{1,0:T(8,128)(2,1)} %ld_ref.1), custom_call_target="tpu_custom_call" | custom-call | flops 67108864 | bytes 3145728 | tf_op jit(solution)/shard_map/pallas_call | solution.py:246
  18.7 2.0 %shard_map.67 = (f32[64,1024]{1,0:T(8,128)S(1)}, f32[64,128]{1,0:T(8,128)S(1)}) custom-call(s32[1,128]{1,0:T(1,128)S(1)} %get-tuple-element.30.firsts_ref, bf16[64,1024]{1,0:T(8,128)(2,1)S(1)} %get-tuple-element.29.after_ref.low_ref, bf16[1024,1024]{1,0:T(8,128)(2,1)S(1)} %get-tuple-element.31.ld_ref, ...), custom_call_target="tpu_custom_call" | custom-call | flops 402653184 | bytes 4194304 | tf_op jit(solution)/shard_map/pallas_call | solution.py:255
  20.6 1.2 %collective-permute-done.1.near_ref = bf16[64,1024]{1,0:T(8,128)(2,1)S(1)} collective-permute-done((bf16[64,1024]{1,0:T(8,128)(2,1)S(1)}, bf16[64,1024]{1,0:T(8,128)(2,1)S(1)}, u32[]{:S(2)}, u32[]{:S(2)}) %collective-permute-start.1) | collective-permute-done | bytes 131104 | tf_op jit(solution)/shard_map/ppermute | solution.py:244
  21.8 0.0 collective-permute-done.far_ref
  21.8 1.0 %shard_map.68 = (f32[64,1024]{1,0:T(8,128)S(1)}, f32[32,128]{1,0:T(8,128)S(1)}) custom-call(s32[1,128]{1,0:T(1,128)S(1)} %get-tuple-element.30.firsts_ref, bf16[64,1024]{1,0:T(8,128)(2,1)S(1)} %collective-permute-done.far_ref, bf16[64,1024]{1,0:T(8,128)(2,1)S(1)} %collective-permute-done.1.near_ref, bf16[1024,1024]{1,0:T(8,128)(2,1)S(1)} %get-tuple-element.31.ld_ref, ...), custom_call_target="tpu_custom_call" | custom-call | tf_op jit(solution)/shard_map/pallas_call | solution.py:268
  22.8 12.1 %all_to_all.34 = f32[32,1,128]{2,1,0:T(1,128)S(1)} all-to-all(f32[32,1,128]{2,1,0:T(1,128)S(1)} %bitcast.18), channel_id=1, replica_groups=mesh['blk'=16,'phe'=2] {'blk','phe'}, dimensions={0} | all-to-all | bytes 32768 | tf_op jit(solution)/shard_map/all_to_all | solution.py:210
  34.9 0.2 shard_map.69
  35.2 0.6 %collective-permute-start.3 = (bf16[64,1024]{1,0:T(8,128)(2,1)S(1)}, bf16[64,1024]{1,0:T(8,128)(2,1)S(1)}, u32[]{:S(2)}, u32[]{:S(2)}) collective-permute-start(bf16[64,1024]{1,0:T(8,128)(2,1)S(1)} %get-tuple-element.37.low_ref), channel_id=1, source_target_pairs={{0,2},{2,0},{4,6},{6,4},{8,10},{10,8},{12,14},{14,12},{16,18},{18,... | collective-permute-start | bytes 393224 | tf_op jit(solution)/shard_map/ppermute | solution.py:244
  35.8 0.7 %collective-permute-start.2 = (bf16[64,1024]{1,0:T(8,128)(2,1)S(1)}, bf16[64,1024]{1,0:T(8,128)(2,1)S(1)}, u32[]{:S(2)}, u32[]{:S(2)}) collective-permute-start(bf16[64,1024]{1,0:T(8,128)(2,1)S(1)} %get-tuple-element.37.low_ref), channel_id=1, source_target_pairs={{2,4},{4,2},{6,8},{8,6},{10,12},{12,10},{14,16},{16,14},{18,20},{2... | collective-permute-start | bytes 393224 | tf_op jit(solution)/shard_map/ppermute | solution.py:243
  36.4 2.0 %shard_map.70 = (f32[64,1024]{1,0:T(8,128)S(1)}, f32[64,128]{1,0:T(8,128)S(1)}) custom-call(s32[1,128]{1,0:T(1,128)S(1)} %get-tuple-element.30.firsts_ref, bf16[64,1024]{1,0:T(8,128)(2,1)S(1)} %get-tuple-element.37.low_ref, bf16[1024,1024]{1,0:T(8,128)(2,1)S(1)} %get-tuple-element.31.ld_ref, f32[64,1024]{1,0:T(8,128)S(1)} %get-tuple-element.26.value_ref.beta_hat_ref, ...), custom_call_target="tpu_custom_call" | custom-call | flops 402653184 | bytes 4194304 | tf_op jit(solution)/shard_map/pallas_call | solution.py:255
  38.4 2.8 %collective-permute-done.3.near_ref = bf16[64,1024]{1,0:T(8,128)(2,1)S(1)} collective-permute-done((bf16[64,1024]{1,0:T(8,128)(2,1)S(1)}, bf16[64,1024]{1,0:T(8,128)(2,1)S(1)}, u32[]{:S(2)}, u32[]{:S(2)}) %collective-permute-start.3) | collective-permute-done | bytes 131104 | tf_op jit(solution)/shard_map/ppermute | solution.py:244
  41.2 0.0 collective-permute-done.2.far_ref
  41.2 1.0 %shard_map.71 = (f32[64,1024]{1,0:T(8,128)S(1)}, f32[32,128]{1,0:T(8,128)S(1)}) custom-call(s32[1,128]{1,0:T(1,128)S(1)} %get-tuple-element.30.firsts_ref, bf16[64,1024]{1,0:T(8,128)(2,1)S(1)} %collective-permute-done.2.far_ref, bf16[64,1024]{1,0:T(8,128)(2,1)S(1)} %collective-permute-done.3.near_ref, bf16[1024,1024]{1,0:T(8,128)(2,1)S(1)} %get-tuple-element.31.ld_ref, ...), custom_call_target="tpu_custom_call" | custom-call | tf_op jit(solution)/shard_map/pallas_call | solution.py:268
  42.2 12.1 %all_to_all.35 = f32[32,1,128]{2,1,0:T(1,128)S(1)} all-to-all(f32[32,1,128]{2,1,0:T(1,128)S(1)} %bitcast.17), channel_id=1, replica_groups=mesh['blk'=16,'phe'=2] {'blk','phe'}, dimensions={0} | all-to-all | bytes 32768 | tf_op jit(solution)/shard_map/all_to_all | solution.py:210
  54.3 0.9 %shard_map.72 = f32[64,1024]{1,0:T(8,128)} custom-call(f32[32,128]{1,0:T(8,128)S(1)} %bitcast.14, s32[1,64]{1,0:T(1,128)S(1)} %get-tuple-element.25.sample_size_ref, f32[64,1024]{1,0:T(8,128)S(1)} %get-tuple-element.42.value_ref, f32[64,1024]{1,0:T(8,128)S(1)} %get-tuple-element.27.psi_ref, bf16[3,64,1024]{2,1,0:T(8,128)(2,1)S(1)} %get-tuple-element.28.noise_ref), custom_call_target="tpu_custom_call" | custom-call | tf_op jit(solution)/shard_map/pallas_call | solution.py:230
Async XLA Ops:
  15.8 6.0 %collective-permute-start.1 = (bf16[64,1024]{1,0:T(8,128)(2,1)S(1)}, bf16[64,1024]{1,0:T(8,128)(2,1)S(1)}, u32[]{:S(2)}, u32[]{:S(2)}) collective-permute-start(bf16[64,1024]{1,0:T(8,128)(2,1)S(1)} %get-tuple-element.29.after_ref.low_ref), channel_id=1, source_target_pairs={{0,2},{2,0},{4,6},{6,4},{8,10},{10,8},{12,14},{14,12},{16,18},{18,... | collective-permute-start | bytes 393224 | tf_op jit(solution)/shard_map/ppermute | solution.py:244
  16.4 5.4 %collective-permute-start = (bf16[64,1024]{1,0:T(8,128)(2,1)S(1)}, bf16[64,1024]{1,0:T(8,128)(2,1)S(1)}, u32[]{:S(2)}, u32[]{:S(2)}) collective-permute-start(bf16[64,1024]{1,0:T(8,128)(2,1)S(1)} %get-tuple-element.29.after_ref.low_ref), channel_id=1, source_target_pairs={{2,4},{4,2},{6,8},{8,6},{10,12},{12,10},{14,16},{16,14},{18,20},{2... | collective-permute-start | bytes 393224 | tf_op jit(solution)/shard_map/ppermute | solution.py:243
  35.2 6.0 %collective-permute-start.3 = (bf16[64,1024]{1,0:T(8,128)(2,1)S(1)}, bf16[64,1024]{1,0:T(8,128)(2,1)S(1)}, u32[]{:S(2)}, u32[]{:S(2)}) collective-permute-start(bf16[64,1024]{1,0:T(8,128)(2,1)S(1)} %get-tuple-element.37.low_ref), channel_id=1, source_target_pairs={{0,2},{2,0},{4,6},{6,4},{8,10},{10,8},{12,14},{14,12},{16,18},{18,... | collective-permute-start | bytes 393224 | tf_op jit(solution)/shard_map/ppermute | solution.py:244
  35.8 5.4 %collective-permute-start.2 = (bf16[64,1024]{1,0:T(8,128)(2,1)S(1)}, bf16[64,1024]{1,0:T(8,128)(2,1)S(1)}, u32[]{:S(2)}, u32[]{:S(2)}) collective-permute-start(bf16[64,1024]{1,0:T(8,128)(2,1)S(1)} %get-tuple-element.37.low_ref), channel_id=1, source_target_pairs={{2,4},{4,2},{6,8},{8,6},{10,12},{12,10},{14,16},{16,14},{18,20},{2... | collective-permute-start | bytes 393224 | tf_op jit(solution)/shard_map/ppermute | solution.py:243

commit v3 on v2

--- a/solution.py
+++ b/solution.py
@@ -81,7 +81,7 @@
             low_ref[:, cut] = beta.astype(jnp.bfloat16)
 
 
-def turned(buffer, start, store):
+def turned(buffer, start, width, store):
     phenos = buffer.shape[0]
     whole = pl.multiple_of(lax.div(start, LANES) * LANES, LANES)
     rest = start - whole
@@ -92,14 +92,14 @@
         return pltpu.roll(buffer[:, pl.ds(pl.multiple_of(whole + at, LANES), LANES)].astype(jnp.float32), turn, 1)
 
     now = piece(0)
-    for at in range(0, (buffer.shape[1] - LANES) // 3 // LANES * LANES, LANES):
+    for at in range(0, width, LANES):
         after = piece(at + LANES)
         store(slice(at, at + LANES), jnp.where(keep, now, after).astype(jnp.bfloat16))
         now = after
 
 
-def product_with(low, ld_ref, cut):
-    return lax.dot_general(low, ld_ref[cut], (((1,), (1,)), ((), ())), preferred_element_type=jnp.float32)
+def product_with(low, ld):
+    return lax.dot_general(low, ld, (((1,), (1,)), ((), ())), preferred_element_type=jnp.float32)
 
 
 def inner(along, firsts_ref, low_ref, ld_ref, beta_hat_ref, psi_ref, beta_ref, grad_ref, scale_ref, wide, windows, slots):
@@ -115,7 +115,7 @@
         def store(cut, values):
             windows[slot, :, cut] = values
 
-        turned(wide, first - base + span, store)
+        turned(wide, first - base + span, span, store)
 
     fill(0, firsts_ref[0, 0])
     slots[0] = 0
@@ -137,7 +137,7 @@
     for tile in range(tiles):
         cut = slice(tile * TILE, (tile + 1) * TILE)
         known = [(slots[number], firsts_ref[0, number] - base) for number in range(tile * steps, (tile + 1) * steps)]
-        product = product_with(windows[pl.ds(known[0][0], WINDOWS)].reshape(WINDOWS * phenos, span), ld_ref, cut)
+        product = product_with(windows[pl.ds(known[0][0], WINDOWS)].reshape(WINDOWS * phenos, span), ld_ref[cut])
         row = lax.broadcasted_iota(jnp.int32, (phenos, TILE), 1) + tile * TILE
         applied = product[:phenos]
         for turn in range(1, WINDOWS):
@@ -151,16 +151,17 @@
     scale_ref[...] = scale
 
 
-def outer(along, firsts_ref, far_ref, near_ref, ld_ref, grad_ref, scale_ref, beta_ref, value_ref, out_ref, sides, windows):
+def outer(along, far, firsts_ref, halo_ref, ld_ref, grad_ref, *refs):
     rows, span = ld_ref.shape
-    phenos = far_ref.shape[0]
+    phenos = halo_ref.shape[0]
+    sides, window = refs[-2:]
     place = lax.axis_index(along)
     base = place * rows
-    odd = lax.rem(place, 2) == 1
+    left = lax.rem(place, 2) == (0 if far else 1)
     gap = span + LANES
-    sides[:, span : span + gap] = jnp.zeros((phenos, gap), sides.dtype)
-    sides[:, pl.ds(pl.multiple_of(jnp.where(odd, span + gap, 0), LANES), span)] = far_ref[...]
-    sides[:, pl.ds(pl.multiple_of(jnp.where(odd, 0, span + gap), LANES), span)] = near_ref[...]
+    sides[:, :gap] = jnp.zeros((phenos, gap), sides.dtype)
+    sides[:, gap : gap + span] = halo_ref[...]
+    sides[:, gap + span :] = jnp.zeros((phenos, gap), sides.dtype)
     table = firsts_ref[...]
     count = 2 * rows // LANES
     first = table[0, 0] - base
@@ -168,31 +169,36 @@
     lane = lax.broadcasted_iota(jnp.int32, table.shape, 1)
     ends = jnp.where((lane < count) & (table - base != first), table - base, rows)
     end = jnp.min(ends.astype(jnp.float32), axis=1, keepdims=True).astype(jnp.int32)
-
-    def store_at(begin):
-        def store(cut, values):
-            windows[begin : begin + phenos, cut] = values
-
-        return store
-
-    turned(sides, first + span, store_at(0))
-    turned(sides, jnp.maximum(last, 0) + gap, store_at(phenos))
+    low_row = jnp.where(left, 0, last)
+    high_row = jnp.where(left, end, rows)
+
+    def store(cut, values):
+        window[:, cut] = values
+
+    turned(sides, jnp.where(left, first + span + gap, jnp.maximum(last, 0) + LANES), span, store)
     resid = jnp.zeros((phenos, LANES), jnp.float32)
-    for tile in range(rows // TILE):
-        cut = slice(tile * TILE, (tile + 1) * TILE)
-        product = product_with(windows[...], ld_ref, cut)
-        row = lax.broadcasted_iota(jnp.int32, (phenos, TILE), 1) + tile * TILE
-        applied = jnp.where(row < end, product[:phenos], 0.0) + jnp.where(row >= last, product[phenos:], 0.0)
-        grad = grad_ref[:, cut] - applied
-        value_ref[:, cut] = beta_ref[:, cut] + grad
+    tiles = rows // TILE
+    for turn in range(tiles):
+        width = span - turn * TILE
+        begin = pl.multiple_of(jnp.where(left, turn, tiles - 1 - turn) * TILE, TILE)
+        cut, part = pl.ds(begin, TILE), pl.ds(pl.multiple_of(jnp.where(left, 0, span - width), TILE), width)
+        row = lax.broadcasted_iota(jnp.int32, (phenos, TILE), 1) + begin
+        inside = (row >= low_row) & (row < high_row)
+        grad = grad_ref[:, cut] - jnp.where(inside, product_with(window[:, part], ld_ref[cut, part]), 0.0)
+        if not far:
+            refs[0][:, cut] = grad
+            continue
+        refs[2][:, cut] = refs[1][:, cut] + grad
         resid = resid + chunk_sums(grad * grad)
-    spread(resid, scale_ref[...], out_ref)
+    if far:
+        spread(resid, refs[0][...], refs[3])
 
 
 def shards(ld_rows, block_first, beta_hat, psi, noise, sample_size):
     rows, span = ld_rows.shape
     phenos = beta_hat.shape[0]
     blocks, groups = lax.axis_size("blk"), lax.axis_size("phe")
+    assert rows == span and rows % TILE == 0, rows
     snps = rows * blocks
     every = ("blk", "phe")
     vmem = pl.BlockSpec(memory_space=pltpu.VMEM)
@@ -265,17 +271,24 @@
             compiler_params=params,
             cost_estimate=pl.CostEstimate(flops=2 * WINDOWS * phenos * rows * span, bytes_accessed=4 << 20, transcendentals=0),
         )(firsts, low, ld_rows, beta_hat, psi, beta)
+        sides = [pltpu.VMEM((phenos, 3 * span + 2 * LANES), jnp.bfloat16), pltpu.VMEM((phenos, span), jnp.bfloat16)]
+        grad = pl.pallas_call(
+            functools.partial(outer, "blk", False),
+            in_specs=[vmem] * 4,
+            out_specs=vmem,
+            out_shape=wide_shape,
+            scratch_shapes=sides,
+            compiler_params=params,
+            cost_estimate=pl.CostEstimate(flops=2 * phenos * rows * span, bytes_accessed=3 << 20, transcendentals=0),
+        )(firsts, near_low, ld_rows, grad)
         value, sums = pl.pallas_call(
-            functools.partial(outer, "blk"),
-            in_specs=[vmem] * 7,
+            functools.partial(outer, "blk", True),
+            in_specs=[vmem] * 6,
             out_specs=[vmem] * 2,
             out_shape=[wide_shape, sums_shape],
-            scratch_shapes=[
-                pltpu.VMEM((phenos, 3 * span + LANES), jnp.bfloat16),
-                pltpu.VMEM((2 * phenos, span), jnp.bfloat16),
-            ],
+            scratch_shapes=sides,
             compiler_params=params,
-        )(firsts, far_low, near_low, ld_rows, grad, scale, beta)
+        )(firsts, far_low, ld_rows, grad, scale, beta)
         sums = total(sums)
     return step(ITERS - 1, sums, value)
 

time: 55.5 us -> 54.9 us (0.989)
  blocking collectives: 38.4 us -> 37.1 us
  Pallas kernels: 10.3 us -> 11 us
    all_to_all x3, blocking collectives: 38.4 us -> 37.1 us  [total(): return lax.all_to_all(sums, every, 0, 0, tiled=True)]
    pallas_call x2 -> x4, Pallas kernels: 2.09 us -> 2.83 us  [the longest x2 1.51 us: shards(): pl.pallas_call(functools.partial(outer, 'blk', True), in_specs=[vmem] * 6...]
  transfers between devices with their start and end apart: 4 -> 4, of which waited for: 2 -> 2; matrix products, arithmetic and copies ran while one was open for 0% -> 0% of each run, Pallas kernels for 10% -> 13%
where the time goes in v3:
time: 54.9 us; the launch traced here: 54.7 us
  blocking collectives  37.1 us (68%)
  Pallas kernels  11 us (20%)
  waiting for transfers between devices  3.96 us (7%)
  starting transfers between devices  2.51 us (5%)
    all_to_all x3, blocking collectives, total(): return lax.all_to_all(sums, every, 0, 0, tiled=True)  37.1 us
    ppermute x2, waiting for transfers between devices, shards(): near_low = lax.ppermute(low, 'blk', near)  3.95 us
    pallas_call x2, Pallas kernels, shards(): pl.pallas_call(functools.partial(inner, 'blk'), in_specs=[smem] + [vmem]...  3.93 us
    pallas_call x1, Pallas kernels, shards(): pl.pallas_call(load, in_specs=[vmem] + [hbm] * 2, out_specs=[vmem] * 2, o...  1.63 us
    pallas_call x2, Pallas kernels, shards(): pl.pallas_call(functools.partial(outer, 'blk', True), in_specs=[vmem] * 6...  1.51 us
    pallas_call x3, Pallas kernels, step(): pl.pallas_call(functools.partial(update, 'phe', groups, snps, t), in_spec...  1.42 us
    pallas_call x2, Pallas kernels, shards(): pl.pallas_call(functools.partial(outer, 'blk', False), in_specs=[vmem] *...  1.32 us
    ppermute x2, starting transfers between devices, shards(): far_low = lax.ppermute(low, 'blk', far)  1.31 us
  transfers between devices with their start and end apart: 4, of which 2 were waited for; matrix products, arithmetic and copies ran while one was open for 0% of the time, Pallas kernels for 13%

profile of v3, /device:TPU:0, one launch (start us, length us, event | category | flops | bytes accessed | tf_op | source)
XLA Modules:
  0.0 54.7 jit_solution(16323166920032209037)
XLA Ops:
  0.0 1.2 %shard_map.64 = (f32[64,1024]{1,0:T(8,128)S(1)}, f32[64,1024]{1,0:T(8,128)S(1)}, bf16[3,64,1024]{2,1,0:T(8,128)(2,1)S(1)}, s32[1,64]{1,0:T(1,128)S(1)}, f32[32,128]{1,0:T(8,128)S(1)}) custom-call(f32[64,1024]{1,0:T(8,128)} %beta_hat_ref.1, f32[64,1024]{1,0:T(8,128)} %psi_ref.1, bf16[3,64,1024]{2,1,0:T(8,128)(2,1)} %noise_ref.1, s32[1,64]{1,0:T(1,128)} %bitcast.21), custom_call_target="tpu_custom_call" | custom-call | tf_op jit(solution)/shard_map/pallas_call | solution.py:218
  1.2 14.3 %all_to_all.33 = f32[32,1,128]{2,1,0:T(1,128)S(1)} all-to-all(f32[32,1,128]{2,1,0:T(1,128)S(1)} %bitcast.19), channel_id=1, replica_groups=mesh['blk'=16,'phe'=2] {'blk','phe'}, dimensions={0} | all-to-all | bytes 32768 | tf_op jit(solution)/shard_map/all_to_all | solution.py:216
  15.5 0.2 shard_map.65
  15.8 0.6 %collective-permute-start.1 = (bf16[64,1024]{1,0:T(8,128)(2,1)S(1)}, bf16[64,1024]{1,0:T(8,128)(2,1)S(1)}, u32[]{:S(2)}, u32[]{:S(2)}) collective-permute-start(bf16[64,1024]{1,0:T(8,128)(2,1)S(1)} %get-tuple-element.29.after_ref.low_ref), channel_id=1, source_target_pairs={{0,2},{2,0},{4,6},{6,4},{8,10},{10,8},{12,14},{14,12},{16,18},{18,... | collective-permute-start | bytes 393224 | tf_op jit(solution)/shard_map/ppermute | solution.py:250
  16.4 0.7 %collective-permute-start = (bf16[64,1024]{1,0:T(8,128)(2,1)S(1)}, bf16[64,1024]{1,0:T(8,128)(2,1)S(1)}, u32[]{:S(2)}, u32[]{:S(2)}) collective-permute-start(bf16[64,1024]{1,0:T(8,128)(2,1)S(1)} %get-tuple-element.29.after_ref.low_ref), channel_id=1, source_target_pairs={{2,4},{4,2},{6,8},{8,6},{10,12},{12,10},{14,16},{16,14},{18,20},{2... | collective-permute-start | bytes 393224 | tf_op jit(solution)/shard_map/ppermute | solution.py:249
  17.0 1.6 %shard_map.66 = (bf16[1024,1024]{1,0:T(8,128)(2,1)S(1)}, s32[1,128]{1,0:T(1,128)S(1)}) custom-call(bf16[64,1024]{1,0:T(8,128)(2,1)S(1)} %get-tuple-element.29.after_ref.low_ref, s32[8,128]{1,0:T(8,128)} %bitcast.20, bf16[1024,1024]{1,0:T(8,128)(2,1)} %ld_ref.1), custom_call_target="tpu_custom_call" | custom-call | flops 67108864 | bytes 3145728 | tf_op jit(solution)/shard_map/pallas_call | solution.py:252
  18.7 2.0 %shard_map.67 = (f32[64,1024]{1,0:T(8,128)S(1)}, f32[64,128]{1,0:T(8,128)S(1)}) custom-call(s32[1,128]{1,0:T(1,128)S(1)} %get-tuple-element.30.firsts_ref, bf16[64,1024]{1,0:T(8,128)(2,1)S(1)} %get-tuple-element.29.after_ref.low_ref, bf16[1024,1024]{1,0:T(8,128)(2,1)S(1)} %get-tuple-element.31.ld_ref, ...), custom_call_target="tpu_custom_call" | custom-call | flops 402653184 | bytes 4194304 | tf_op jit(solution)/shard_map/pallas_call | solution.py:261
  20.6 1.2 %collective-permute-done.1.halo_ref = bf16[64,1024]{1,0:T(8,128)(2,1)S(1)} collective-permute-done((bf16[64,1024]{1,0:T(8,128)(2,1)S(1)}, bf16[64,1024]{1,0:T(8,128)(2,1)S(1)}, u32[]{:S(2)}, u32[]{:S(2)}) %collective-permute-start.1) | collective-permute-done | bytes 131104 | tf_op jit(solution)/shard_map/ppermute | solution.py:250
  21.8 0.7 %shard_map.68.grad_ref = f32[64,1024]{1,0:T(8,128)S(1)} custom-call(s32[1,128]{1,0:T(1,128)S(1)} %get-tuple-element.30.firsts_ref, bf16[64,1024]{1,0:T(8,128)(2,1)S(1)} %collective-permute-done.1.halo_ref, bf16[1024,1024]{1,0:T(8,128)(2,1)S(1)} %get-tuple-element.31.ld_ref, f32[64,1024]{1,0:T(8,128)S(1)} %get-tuple-element.33.grad_ref), custom_call_target="tpu_custom_call" | custom-call | flops 134217728 | bytes 3145728 | tf_op jit(solution)/shard_map/pallas_call | solution.py:275
  22.5 0.0 collective-permute-done.halo_ref
  22.5 0.8 %shard_map.69 = (f32[64,1024]{1,0:T(8,128)S(1)}, f32[32,128]{1,0:T(8,128)S(1)}) custom-call(s32[1,128]{1,0:T(1,128)S(1)} %get-tuple-element.30.firsts_ref, bf16[64,1024]{1,0:T(8,128)(2,1)S(1)} %collective-permute-done.halo_ref, bf16[1024,1024]{1,0:T(8,128)(2,1)S(1)} %get-tuple-element.31.ld_ref, f32[64,1024]{1,0:T(8,128)S(1)} %shard_map.68.grad_ref, ...), custom_call_target="tpu_custom_call" | custom-call | tf_op jit(solution)/shard_map/pallas_call | solution.py:284
  23.2 11.4 %all_to_all.34 = f32[32,1,128]{2,1,0:T(1,128)S(1)} all-to-all(f32[32,1,128]{2,1,0:T(1,128)S(1)} %bitcast.18), channel_id=1, replica_groups=mesh['blk'=16,'phe'=2] {'blk','phe'}, dimensions={0} | all-to-all | bytes 32768 | tf_op jit(solution)/shard_map/all_to_all | solution.py:216
  34.6 0.2 shard_map.70
  34.9 0.6 %collective-permute-start.3 = (bf16[64,1024]{1,0:T(8,128)(2,1)S(1)}, bf16[64,1024]{1,0:T(8,128)(2,1)S(1)}, u32[]{:S(2)}, u32[]{:S(2)}) collective-permute-start(bf16[64,1024]{1,0:T(8,128)(2,1)S(1)} %get-tuple-element.37.low_ref), channel_id=1, source_target_pairs={{0,2},{2,0},{4,6},{6,4},{8,10},{10,8},{12,14},{14,12},{16,18},{18,... | collective-permute-start | bytes 393224 | tf_op jit(solution)/shard_map/ppermute | solution.py:250
  35.5 0.7 %collective-permute-start.2 = (bf16[64,1024]{1,0:T(8,128)(2,1)S(1)}, bf16[64,1024]{1,0:T(8,128)(2,1)S(1)}, u32[]{:S(2)}, u32[]{:S(2)}) collective-permute-start(bf16[64,1024]{1,0:T(8,128)(2,1)S(1)} %get-tuple-element.37.low_ref), channel_id=1, source_target_pairs={{2,4},{4,2},{6,8},{8,6},{10,12},{12,10},{14,16},{16,14},{18,20},{2... | collective-permute-start | bytes 393224 | tf_op jit(solution)/shard_map/ppermute | solution.py:249
  36.1 2.0 %shard_map.71 = (f32[64,1024]{1,0:T(8,128)S(1)}, f32[64,128]{1,0:T(8,128)S(1)}) custom-call(s32[1,128]{1,0:T(1,128)S(1)} %get-tuple-element.30.firsts_ref, bf16[64,1024]{1,0:T(8,128)(2,1)S(1)} %get-tuple-element.37.low_ref, bf16[1024,1024]{1,0:T(8,128)(2,1)S(1)} %get-tuple-element.31.ld_ref, f32[64,1024]{1,0:T(8,128)S(1)} %get-tuple-element.26.value_ref.beta_hat_ref, ...), custom_call_target="tpu_custom_call" | custom-call | flops 402653184 | bytes 4194304 | tf_op jit(solution)/shard_map/pallas_call | solution.py:261
  38.1 2.8 %collective-permute-done.3.halo_ref = bf16[64,1024]{1,0:T(8,128)(2,1)S(1)} collective-permute-done((bf16[64,1024]{1,0:T(8,128)(2,1)S(1)}, bf16[64,1024]{1,0:T(8,128)(2,1)S(1)}, u32[]{:S(2)}, u32[]{:S(2)}) %collective-permute-start.3) | collective-permute-done | bytes 131104 | tf_op jit(solution)/shard_map/ppermute | solution.py:250
  40.9 0.7 %shard_map.72.grad_ref = f32[64,1024]{1,0:T(8,128)S(1)} custom-call(s32[1,128]{1,0:T(1,128)S(1)} %get-tuple-element.30.firsts_ref, bf16[64,1024]{1,0:T(8,128)(2,1)S(1)} %collective-permute-done.3.halo_ref, bf16[1024,1024]{1,0:T(8,128)(2,1)S(1)} %get-tuple-element.31.ld_ref, f32[64,1024]{1,0:T(8,128)S(1)} %get-tuple-element.39.grad_ref), custom_call_target="tpu_custom_call" | custom-call | flops 134217728 | bytes 3145728 | tf_op jit(solution)/shard_map/pallas_call | solution.py:275
  41.6 0.0 collective-permute-done.2.halo_ref
  41.6 0.8 %shard_map.73 = (f32[64,1024]{1,0:T(8,128)S(1)}, f32[32,128]{1,0:T(8,128)S(1)}) custom-call(s32[1,128]{1,0:T(1,128)S(1)} %get-tuple-element.30.firsts_ref, bf16[64,1024]{1,0:T(8,128)(2,1)S(1)} %collective-permute-done.2.halo_ref, bf16[1024,1024]{1,0:T(8,128)(2,1)S(1)} %get-tuple-element.31.ld_ref, f32[64,1024]{1,0:T(8,128)S(1)} %shard_map.72.grad_ref, ...), custom_call_target="tpu_custom_call" | custom-call | tf_op jit(solution)/shard_map/pallas_call | solution.py:284
  42.3 11.4 %all_to_all.35 = f32[32,1,128]{2,1,0:T(1,128)S(1)} all-to-all(f32[32,1,128]{2,1,0:T(1,128)S(1)} %bitcast.17), channel_id=1, replica_groups=mesh['blk'=16,'phe'=2] {'blk','phe'}, dimensions={0} | all-to-all | bytes 32768 | tf_op jit(solution)/shard_map/all_to_all | solution.py:216
  53.7 0.9 %shard_map.74 = f32[64,1024]{1,0:T(8,128)} custom-call(f32[32,128]{1,0:T(8,128)S(1)} %bitcast.14, s32[1,64]{1,0:T(1,128)S(1)} %get-tuple-element.25.sample_size_ref, f32[64,1024]{1,0:T(8,128)S(1)} %get-tuple-element.42.value_ref, f32[64,1024]{1,0:T(8,128)S(1)} %get-tuple-element.27.psi_ref, bf16[3,64,1024]{2,1,0:T(8,128)(2,1)S(1)} %get-tuple-element.28.noise_ref), custom_call_target="tpu_custom_call" | custom-call | tf_op jit(solution)/shard_map/pallas_call | solution.py:236
Async XLA Ops:
  15.8 6.0 %collective-permute-start.1 = (bf16[64,1024]{1,0:T(8,128)(2,1)S(1)}, bf16[64,1024]{1,0:T(8,128)(2,1)S(1)}, u32[]{:S(2)}, u32[]{:S(2)}) collective-permute-start(bf16[64,1024]{1,0:T(8,128)(2,1)S(1)} %get-tuple-element.29.after_ref.low_ref), channel_id=1, source_target_pairs={{0,2},{2,0},{4,6},{6,4},{8,10},{10,8},{12,14},{14,12},{16,18},{18,... | collective-permute-start | bytes 393224 | tf_op jit(solution)/shard_map/ppermute | solution.py:250
  16.4 6.1 %collective-permute-start = (bf16[64,1024]{1,0:T(8,128)(2,1)S(1)}, bf16[64,1024]{1,0:T(8,128)(2,1)S(1)}, u32[]{:S(2)}, u32[]{:S(2)}) collective-permute-start(bf16[64,1024]{1,0:T(8,128)(2,1)S(1)} %get-tuple-element.29.after_ref.low_ref), channel_id=1, source_target_pairs={{2,4},{4,2},{6,8},{8,6},{10,12},{12,10},{14,16},{16,14},{18,20},{2... | collective-permute-start | bytes 393224 | tf_op jit(solution)/shard_map/ppermute | solution.py:249
  34.9 6.0 %collective-permute-start.3 = (bf16[64,1024]{1,0:T(8,128)(2,1)S(1)}, bf16[64,1024]{1,0:T(8,128)(2,1)S(1)}, u32[]{:S(2)}, u32[]{:S(2)}) collective-permute-start(bf16[64,1024]{1,0:T(8,128)(2,1)S(1)} %get-tuple-element.37.low_ref), channel_id=1, source_target_pairs={{0,2},{2,0},{4,6},{6,4},{8,10},{10,8},{12,14},{14,12},{16,18},{18,... | collective-permute-start | bytes 393224 | tf_op jit(solution)/shard_map/ppermute | solution.py:250
  35.5 6.1 %collective-permute-start.2 = (bf16[64,1024]{1,0:T(8,128)(2,1)S(1)}, bf16[64,1024]{1,0:T(8,128)(2,1)S(1)}, u32[]{:S(2)}, u32[]{:S(2)}) collective-permute-start(bf16[64,1024]{1,0:T(8,128)(2,1)S(1)} %get-tuple-element.37.low_ref), channel_id=1, source_target_pairs={{2,4},{4,2},{6,8},{8,6},{10,12},{12,10},{14,16},{16,14},{18,20},{2... | collective-permute-start | bytes 393224 | tf_op jit(solution)/shard_map/ppermute | solution.py:249

commit v4 on v3

--- a/solution.py
+++ b/solution.py
@@ -81,7 +81,7 @@
             low_ref[:, cut] = beta.astype(jnp.bfloat16)
 
 
-def turned(buffer, start, width, store):
+def turned(buffer, start, width, store, inside=None):
     phenos = buffer.shape[0]
     whole = pl.multiple_of(lax.div(start, LANES) * LANES, LANES)
     rest = start - whole
@@ -94,7 +94,9 @@
     now = piece(0)
     for at in range(0, width, LANES):
         after = piece(at + LANES)
-        store(slice(at, at + LANES), jnp.where(keep, now, after).astype(jnp.bfloat16))
+        values = jnp.where(keep, now, after)
+        values = values if inside is None else jnp.where(inside, values, 0.0)
+        store(slice(at, at + LANES), values.astype(jnp.bfloat16))
         now = after
 
 
@@ -192,6 +194,56 @@
         resid = resid + chunk_sums(grad * grad)
     if far:
         spread(resid, refs[0][...], refs[3])
+
+
+def align(along, firsts_ref, ld_ref, out_ref, wide):
+    rows, span = ld_ref.shape
+    place = lax.axis_index(along)
+    base = place * rows
+    left = lax.rem(place, 2) == 0
+    gap = span + LANES
+    table = firsts_ref[...]
+    count = 2 * rows // LANES
+    first = table[0, 0] - base
+    last = table[0, count - 1] - base
+    lane = lax.broadcasted_iota(jnp.int32, table.shape, 1)
+    ends = jnp.where((lane < count) & (table - base != first), table - base, rows)
+    end = jnp.min(ends.astype(jnp.float32), axis=1, keepdims=True).astype(jnp.int32)
+    low_row = jnp.where(left, 0, last)
+    high_row = jnp.where(left, end, rows)
+    start = jnp.where(left, gap - first - span, gap + span - jnp.maximum(last, 0))
+    wide[:, :gap] = jnp.zeros((TILE, gap), wide.dtype)
+    wide[:, gap + span :] = jnp.zeros((TILE, gap), wide.dtype)
+
+    tiles = rows // TILE
+    for turn in range(tiles):
+        width = span - turn * TILE
+        begin = pl.multiple_of(jnp.where(left, turn, tiles - 1 - turn) * TILE, TILE)
+        side = pl.multiple_of(jnp.where(left, span - width, 0), TILE)
+        row = lax.broadcasted_iota(jnp.int32, (TILE, LANES), 0) + begin
+        inside = (row >= low_row) & (row < high_row)
+        wide[:, gap : gap + span] = ld_ref[pl.ds(begin, TILE)]
+
+        def store(cut, values, begin=begin, side=side):
+            out_ref[pl.ds(begin, TILE), pl.ds(pl.multiple_of(side + cut.start, LANES), LANES)] = values
+
+        turned(wide, start + side, width, store, inside)
+
+
+def finish(along, halo_ref, far_ld_ref, grad_ref, scale_ref, beta_ref, value_ref, out_ref):
+    rows, span = far_ld_ref.shape
+    phenos = halo_ref.shape[0]
+    left = lax.rem(lax.axis_index(along), 2) == 0
+    resid = jnp.zeros((phenos, LANES), jnp.float32)
+    tiles = rows // TILE
+    for turn in range(tiles):
+        width = span - turn * TILE
+        begin = pl.multiple_of(jnp.where(left, turn, tiles - 1 - turn) * TILE, TILE)
+        cut, part = pl.ds(begin, TILE), pl.ds(pl.multiple_of(jnp.where(left, span - width, 0), TILE), width)
+        grad = grad_ref[:, cut] - product_with(halo_ref[:, part], far_ld_ref[cut, part])
+        value_ref[:, cut] = beta_ref[:, cut] + grad
+        resid = resid + chunk_sums(grad * grad)
+    spread(resid, scale_ref[...], out_ref)
 
 
 def shards(ld_rows, block_first, beta_hat, psi, noise, sample_size):
@@ -281,14 +333,23 @@
             compiler_params=params,
             cost_estimate=pl.CostEstimate(flops=2 * phenos * rows * span, bytes_accessed=3 << 20, transcendentals=0),
         )(firsts, near_low, ld_rows, grad)
+        if t == 0:
+            far_ld = pl.pallas_call(
+                functools.partial(align, "blk"),
+                in_specs=[vmem] * 2,
+                out_specs=vmem,
+                out_shape=pltpu.VMEM(ld_rows.shape, ld_rows.dtype),
+                scratch_shapes=[pltpu.VMEM((TILE, 3 * span + 2 * LANES), jnp.bfloat16)],
+                compiler_params=params,
+                cost_estimate=pl.CostEstimate(flops=1 << 26, bytes_accessed=4 << 20, transcendentals=0),
+            )(firsts, ld_rows)
         value, sums = pl.pallas_call(
-            functools.partial(outer, "blk", True),
-            in_specs=[vmem] * 6,
+            functools.partial(finish, "blk"),
+            in_specs=[vmem] * 5,
             out_specs=[vmem] * 2,
             out_shape=[wide_shape, sums_shape],
-            scratch_shapes=sides,
             compiler_params=params,
-        )(firsts, far_low, ld_rows, grad, scale, beta)
+        )(far_low, far_ld, grad, scale, beta)
         sums = total(sums)
     return step(ITERS - 1, sums, value)
 

time: 54.9 us -> 54.7 us (level)
  waiting for transfers between devices: 3.96 us -> 2.95 us
  Pallas kernels: 11 us -> 11.7 us
    ppermute x2, waiting for transfers between devices: 3.95 us -> 2.95 us  [shards(): near_low = lax.ppermute(low, 'blk', near)]
    pallas_call x2 -> x3, Pallas kernels: 1.51 us -> 2.26 us  [the longest x2 1.26 us: shards(): pl.pallas_call(functools.partial(finish, 'blk'), in_specs=[vmem] * 5, out...]
  transfers between devices with their start and end apart: 4 -> 4, of which waited for: 2 -> 2; matrix products, arithmetic and copies ran while one was open for 0% -> 0% of each run, Pallas kernels for 13% -> 14%
where the time goes in v4:
time: 54.7 us; the launch traced here: 54.5 us
  blocking collectives  37.2 us (68%)
  Pallas kernels  11.7 us (21%)
  waiting for transfers between devices  2.95 us (5%)
  starting transfers between devices  2.51 us (5%)
    all_to_all x3, blocking collectives, total(): return lax.all_to_all(sums, every, 0, 0, tiled=True)  37.2 us
    pallas_call x2, Pallas kernels, shards(): pl.pallas_call(functools.partial(inner, 'blk'), in_specs=[smem] + [vmem]...  3.93 us
    ppermute x2, waiting for transfers between devices, shards(): near_low = lax.ppermute(low, 'blk', near)  2.95 us
    pallas_call x1, Pallas kernels, shards(): pl.pallas_call(load, in_specs=[vmem] + [hbm] * 2, out_specs=[vmem] * 2, o...  1.63 us
    pallas_call x3, Pallas kernels, step(): pl.pallas_call(functools.partial(update, 'phe', groups, snps, t), in_spec...  1.42 us
    pallas_call x2, Pallas kernels, shards(): pl.pallas_call(functools.partial(outer, 'blk', False), in_specs=[vmem] *...  1.32 us
    ppermute x2, starting transfers between devices, shards(): far_low = lax.ppermute(low, 'blk', far)  1.31 us
    pallas_call x2, Pallas kernels, shards(): pl.pallas_call(functools.partial(finish, 'blk'), in_specs=[vmem] * 5, out...  1.26 us
  transfers between devices with their start and end apart: 4, of which 2 were waited for; matrix products, arithmetic and copies ran while one was open for 0% of the time, Pallas kernels for 14%

profile of v4, /device:TPU:0, one launch (start us, length us, event | category | flops | bytes accessed | tf_op | source)
XLA Modules:
  0.0 54.5 jit_solution(8485334820909231531)
XLA Ops:
  0.0 1.2 %shard_map.64 = (f32[64,1024]{1,0:T(8,128)S(1)}, f32[64,1024]{1,0:T(8,128)S(1)}, bf16[3,64,1024]{2,1,0:T(8,128)(2,1)S(1)}, s32[1,64]{1,0:T(1,128)S(1)}, f32[32,128]{1,0:T(8,128)S(1)}) custom-call(f32[64,1024]{1,0:T(8,128)} %beta_hat_ref.1, f32[64,1024]{1,0:T(8,128)} %psi_ref.1, bf16[3,64,1024]{2,1,0:T(8,128)(2,1)} %noise_ref.1, s32[1,64]{1,0:T(1,128)} %bitcast.21), custom_call_target="tpu_custom_call" | custom-call | tf_op jit(solution)/shard_map/pallas_call | solution.py:270
  1.2 14.3 %all_to_all.33 = f32[32,1,128]{2,1,0:T(1,128)S(1)} all-to-all(f32[32,1,128]{2,1,0:T(1,128)S(1)} %bitcast.19), channel_id=1, replica_groups=mesh['blk'=16,'phe'=2] {'blk','phe'}, dimensions={0} | all-to-all | bytes 32768 | tf_op jit(solution)/shard_map/all_to_all | solution.py:268
  15.5 0.2 shard_map.65
  15.8 0.6 %collective-permute-start.1 = (bf16[64,1024]{1,0:T(8,128)(2,1)S(1)}, bf16[64,1024]{1,0:T(8,128)(2,1)S(1)}, u32[]{:S(2)}, u32[]{:S(2)}) collective-permute-start(bf16[64,1024]{1,0:T(8,128)(2,1)S(1)} %get-tuple-element.29.after_ref.low_ref), channel_id=1, source_target_pairs={{0,2},{2,0},{4,6},{6,4},{8,10},{10,8},{12,14},{14,12},{16,18},{18,... | collective-permute-start | bytes 393224 | tf_op jit(solution)/shard_map/ppermute | solution.py:302
  16.4 0.7 %collective-permute-start = (bf16[64,1024]{1,0:T(8,128)(2,1)S(1)}, bf16[64,1024]{1,0:T(8,128)(2,1)S(1)}, u32[]{:S(2)}, u32[]{:S(2)}) collective-permute-start(bf16[64,1024]{1,0:T(8,128)(2,1)S(1)} %get-tuple-element.29.after_ref.low_ref), channel_id=1, source_target_pairs={{2,4},{4,2},{6,8},{8,6},{10,12},{12,10},{14,16},{16,14},{18,20},{2... | collective-permute-start | bytes 393224 | tf_op jit(solution)/shard_map/ppermute | solution.py:301
  17.0 1.6 %shard_map.66 = (bf16[1024,1024]{1,0:T(8,128)(2,1)S(1)}, s32[1,128]{1,0:T(1,128)S(1)}) custom-call(bf16[64,1024]{1,0:T(8,128)(2,1)S(1)} %get-tuple-element.29.after_ref.low_ref, s32[8,128]{1,0:T(8,128)} %bitcast.20, bf16[1024,1024]{1,0:T(8,128)(2,1)} %ld_ref.1), custom_call_target="tpu_custom_call" | custom-call | flops 67108864 | bytes 3145728 | tf_op jit(solution)/shard_map/pallas_call | solution.py:304
  18.7 1.0 %shard_map.67.far_ld_ref = bf16[1024,1024]{1,0:T(8,128)(2,1)S(1)} custom-call(s32[1,128]{1,0:T(1,128)S(1)} %get-tuple-element.30.firsts_ref, bf16[1024,1024]{1,0:T(8,128)(2,1)S(1)} %get-tuple-element.31.ld_ref), custom_call_target="tpu_custom_call" | custom-call | flops 67108864 | bytes 4194304 | tf_op jit(solution)/shard_map/pallas_call | solution.py:337
  19.7 2.0 %shard_map.68 = (f32[64,1024]{1,0:T(8,128)S(1)}, f32[64,128]{1,0:T(8,128)S(1)}) custom-call(s32[1,128]{1,0:T(1,128)S(1)} %get-tuple-element.30.firsts_ref, bf16[64,1024]{1,0:T(8,128)(2,1)S(1)} %get-tuple-element.29.after_ref.low_ref, bf16[1024,1024]{1,0:T(8,128)(2,1)S(1)} %get-tuple-element.31.ld_ref, ...), custom_call_target="tpu_custom_call" | custom-call | flops 402653184 | bytes 4194304 | tf_op jit(solution)/shard_map/pallas_call | solution.py:313
  21.6 0.2 collective-permute-done.1.halo_ref
  21.8 0.7 %shard_map.69.grad_ref = f32[64,1024]{1,0:T(8,128)S(1)} custom-call(s32[1,128]{1,0:T(1,128)S(1)} %get-tuple-element.30.firsts_ref, bf16[64,1024]{1,0:T(8,128)(2,1)S(1)} %collective-permute-done.1.halo_ref, bf16[1024,1024]{1,0:T(8,128)(2,1)S(1)} %get-tuple-element.31.ld_ref, f32[64,1024]{1,0:T(8,128)S(1)} %get-tuple-element.33.grad_ref), custom_call_target="tpu_custom_call" | custom-call | flops 134217728 | bytes 3145728 | tf_op jit(solution)/shard_map/pallas_call | solution.py:327
  22.5 0.0 collective-permute-done.halo_ref
  22.5 0.6 %shard_map.70 = (f32[64,1024]{1,0:T(8,128)S(1)}, f32[32,128]{1,0:T(8,128)S(1)}) custom-call(bf16[64,1024]{1,0:T(8,128)(2,1)S(1)} %collective-permute-done.halo_ref, bf16[1024,1024]{1,0:T(8,128)(2,1)S(1)} %shard_map.67.far_ld_ref, f32[64,1024]{1,0:T(8,128)S(1)} %shard_map.69.grad_ref, f32[64,128]{1,0:T(8,128)S(1)} %get-tuple-element.34.scale_ref, ...), custom_call_target="tpu_custom_call" | custom-call | tf_op jit(solution)/shard_map/pallas_call | solution.py:346
  23.1 11.5 %all_to_all.34 = f32[32,1,128]{2,1,0:T(1,128)S(1)} all-to-all(f32[32,1,128]{2,1,0:T(1,128)S(1)} %bitcast.18), channel_id=1, replica_groups=mesh['blk'=16,'phe'=2] {'blk','phe'}, dimensions={0} | all-to-all | bytes 32768 | tf_op jit(solution)/shard_map/all_to_all | solution.py:268
  34.6 0.2 shard_map.71
  34.9 0.6 %collective-permute-start.3 = (bf16[64,1024]{1,0:T(8,128)(2,1)S(1)}, bf16[64,1024]{1,0:T(8,128)(2,1)S(1)}, u32[]{:S(2)}, u32[]{:S(2)}) collective-permute-start(bf16[64,1024]{1,0:T(8,128)(2,1)S(1)} %get-tuple-element.37.low_ref), channel_id=1, source_target_pairs={{0,2},{2,0},{4,6},{6,4},{8,10},{10,8},{12,14},{14,12},{16,18},{18,... | collective-permute-start | bytes 393224 | tf_op jit(solution)/shard_map/ppermute | solution.py:302
  35.5 0.7 %collective-permute-start.2 = (bf16[64,1024]{1,0:T(8,128)(2,1)S(1)}, bf16[64,1024]{1,0:T(8,128)(2,1)S(1)}, u32[]{:S(2)}, u32[]{:S(2)}) collective-permute-start(bf16[64,1024]{1,0:T(8,128)(2,1)S(1)} %get-tuple-element.37.low_ref), channel_id=1, source_target_pairs={{2,4},{4,2},{6,8},{8,6},{10,12},{12,10},{14,16},{16,14},{18,20},{2... | collective-permute-start | bytes 393224 | tf_op jit(solution)/shard_map/ppermute | solution.py:301
  36.1 2.0 %shard_map.72 = (f32[64,1024]{1,0:T(8,128)S(1)}, f32[64,128]{1,0:T(8,128)S(1)}) custom-call(s32[1,128]{1,0:T(1,128)S(1)} %get-tuple-element.30.firsts_ref, bf16[64,1024]{1,0:T(8,128)(2,1)S(1)} %get-tuple-element.37.low_ref, bf16[1024,1024]{1,0:T(8,128)(2,1)S(1)} %get-tuple-element.31.ld_ref, f32[64,1024]{1,0:T(8,128)S(1)} %get-tuple-element.26.value_ref.beta_hat_ref, ...), custom_call_target="tpu_custom_call" | custom-call | flops 402653184 | bytes 4194304 | tf_op jit(solution)/shard_map/pallas_call | solution.py:313
  38.1 2.8 %collective-permute-done.3.halo_ref = bf16[64,1024]{1,0:T(8,128)(2,1)S(1)} collective-permute-done((bf16[64,1024]{1,0:T(8,128)(2,1)S(1)}, bf16[64,1024]{1,0:T(8,128)(2,1)S(1)}, u32[]{:S(2)}, u32[]{:S(2)}) %collective-permute-start.3) | collective-permute-done | bytes 131104 | tf_op jit(solution)/shard_map/ppermute | solution.py:302
  40.9 0.7 %shard_map.73.grad_ref = f32[64,1024]{1,0:T(8,128)S(1)} custom-call(s32[1,128]{1,0:T(1,128)S(1)} %get-tuple-element.30.firsts_ref, bf16[64,1024]{1,0:T(8,128)(2,1)S(1)} %collective-permute-done.3.halo_ref, bf16[1024,1024]{1,0:T(8,128)(2,1)S(1)} %get-tuple-element.31.ld_ref, f32[64,1024]{1,0:T(8,128)S(1)} %get-tuple-element.39.grad_ref), custom_call_target="tpu_custom_call" | custom-call | flops 134217728 | bytes 3145728 | tf_op jit(solution)/shard_map/pallas_call | solution.py:327
  41.6 0.0 collective-permute-done.2.halo_ref
  41.6 0.6 %shard_map.74 = (f32[64,1024]{1,0:T(8,128)S(1)}, f32[32,128]{1,0:T(8,128)S(1)}) custom-call(bf16[64,1024]{1,0:T(8,128)(2,1)S(1)} %collective-permute-done.2.halo_ref, bf16[1024,1024]{1,0:T(8,128)(2,1)S(1)} %shard_map.67.far_ld_ref, f32[64,1024]{1,0:T(8,128)S(1)} %shard_map.73.grad_ref, f32[64,128]{1,0:T(8,128)S(1)} %get-tuple-element.40.scale_ref, ...), custom_call_target="tpu_custom_call" | custom-call | tf_op jit(solution)/shard_map/pallas_call | solution.py:346
  42.2 11.4 %all_to_all.35 = f32[32,1,128]{2,1,0:T(1,128)S(1)} all-to-all(f32[32,1,128]{2,1,0:T(1,128)S(1)} %bitcast.17), channel_id=1, replica_groups=mesh['blk'=16,'phe'=2] {'blk','phe'}, dimensions={0} | all-to-all | bytes 32768 | tf_op jit(solution)/shard_map/all_to_all | solution.py:268
  53.6 0.9 %shard_map.75 = f32[64,1024]{1,0:T(8,128)} custom-call(f32[32,128]{1,0:T(8,128)S(1)} %bitcast.14, s32[1,64]{1,0:T(1,128)S(1)} %get-tuple-element.25.sample_size_ref, f32[64,1024]{1,0:T(8,128)S(1)} %get-tuple-element.42.value_ref, f32[64,1024]{1,0:T(8,128)S(1)} %get-tuple-element.27.psi_ref, bf16[3,64,1024]{2,1,0:T(8,128)(2,1)S(1)} %get-tuple-element.28.noise_ref), custom_call_target="tpu_custom_call" | custom-call | tf_op jit(solution)/shard_map/pallas_call | solution.py:288
Async XLA Ops:
  15.8 6.0 %collective-permute-start.1 = (bf16[64,1024]{1,0:T(8,128)(2,1)S(1)}, bf16[64,1024]{1,0:T(8,128)(2,1)S(1)}, u32[]{:S(2)}, u32[]{:S(2)}) collective-permute-start(bf16[64,1024]{1,0:T(8,128)(2,1)S(1)} %get-tuple-element.29.after_ref.low_ref), channel_id=1, source_target_pairs={{0,2},{2,0},{4,6},{6,4},{8,10},{10,8},{12,14},{14,12},{16,18},{18,... | collective-permute-start | bytes 393224 | tf_op jit(solution)/shard_map/ppermute | solution.py:302
  16.4 6.1 %collective-permute-start = (bf16[64,1024]{1,0:T(8,128)(2,1)S(1)}, bf16[64,1024]{1,0:T(8,128)(2,1)S(1)}, u32[]{:S(2)}, u32[]{:S(2)}) collective-permute-start(bf16[64,1024]{1,0:T(8,128)(2,1)S(1)} %get-tuple-element.29.after_ref.low_ref), channel_id=1, source_target_pairs={{2,4},{4,2},{6,8},{8,6},{10,12},{12,10},{14,16},{16,14},{18,20},{2... | collective-permute-start | bytes 393224 | tf_op jit(solution)/shard_map/ppermute | solution.py:301
  34.9 6.0 %collective-permute-start.3 = (bf16[64,1024]{1,0:T(8,128)(2,1)S(1)}, bf16[64,1024]{1,0:T(8,128)(2,1)S(1)}, u32[]{:S(2)}, u32[]{:S(2)}) collective-permute-start(bf16[64,1024]{1,0:T(8,128)(2,1)S(1)} %get-tuple-element.37.low_ref), channel_id=1, source_target_pairs={{0,2},{2,0},{4,6},{6,4},{8,10},{10,8},{12,14},{14,12},{16,18},{18,... | collective-permute-start | bytes 393224 | tf_op jit(solution)/shard_map/ppermute | solution.py:302
  35.5 6.1 %collective-permute-start.2 = (bf16[64,1024]{1,0:T(8,128)(2,1)S(1)}, bf16[64,1024]{1,0:T(8,128)(2,1)S(1)}, u32[]{:S(2)}, u32[]{:S(2)}) collective-permute-start(bf16[64,1024]{1,0:T(8,128)(2,1)S(1)} %get-tuple-element.37.low_ref), channel_id=1, source_target_pairs={{2,4},{4,2},{6,8},{8,6},{10,12},{12,10},{14,16},{16,14},{18,20},{2... | collective-permute-start | bytes 393224 | tf_op jit(solution)/shard_map/ppermute | solution.py:301
